TPU v7x, 128 devices: a whole 4x4x4 slice. The times are simulated.
128 devices in a mesh: dp: 32 (over x, y, core), mp: 4 (over z).
Axes of the slice: x: 4, y: 4, z: 4, core: 2. Of those that a mesh axis runs over, the one named last changes fastest.
Arguments:
- tokens: bfloat16 [49152, 4096], P('dp'), may hold values from -40 to 40
- norm_gain: bfloat16 [4096], replicated, may hold values from 0.099609375 to 1.8984375
- w_query: bfloat16 [4096, 2048], P(None, 'mp'), may hold values from -1 to 1
- w_key: bfloat16 [4096, 512], P(None, 'mp'), may hold values from -4 to 4
- w_value: bfloat16 [4096, 512], P(None, 'mp'), may hold values from -0.09375 to 0.09375
- w_out: bfloat16 [2048, 4096], P('mp'), may hold values from -0.125 to 0.125
- seq_starts: int32 [256], P('dp'), may hold values from 0 to 1408, as said below
- seq_lengths: int32 [256], P('dp'), may hold values from 128 to 640
- episode_ids: int32 [256], replicated, may hold values from 0 to 3, as said below
- class_ids: int32 [256], replicated, may hold values from 0 to 31
- query_flags: int32 [256], replicated, may hold values from 0 to 1
Outputs:
- log_probs: float32 [256, 32], P('dp')
- prototypes: float32 [128, 4096], P(None, 'mp')
Inputs may be any that keep to these rules, and one draw needn't show every extreme that they name: `seq_starts`: slot s lies in the buffer of dp index s // 8; the slots of one buffer are disjoint and in increasing order of start; start plus length is at most 1536, and in every draw the last slot of some buffer ends at row 1536. `episode_ids`: every class of every episode has at least one support sequence.
All inputs are finite; a program needn't handle non-finite values.
Results may differ from a plain program's by a relative error of at most 0.004.
Values sent between devices are 32-bit elements; how exact they have to be, the bound alone decides.
A program may use at most 128 MiB of HBM per device.

v0:
```python
import math

import jax
import jax.numpy as jnp
from jax import lax
from jax.sharding import PartitionSpec as P

HEAD_DIM = 128
WAYS = 32


ROPE_BASE = 500000.0
NEG_FILL = -1e30


def sent_to_all(array, axis):
    copies = jnp.broadcast_to(array, (lax.axis_size(axis), *array.shape))
    return lax.all_to_all(copies, axis, split_axis=0, concat_axis=0, tiled=True)


def taken_together(array, axis):
    return sent_to_all(array, axis).sum(axis=0)


def rotate(vectors, positions):
    half_dim = vectors.shape[-1] // 2
    frequency = jnp.power(
        ROPE_BASE, -(jnp.arange(half_dim, dtype=jnp.float32) * 2.0 / vectors.shape[-1])
    )
    angles = positions.astype(jnp.float32)[:, None] * frequency[None, :]
    cosine = jnp.cos(angles)[:, None, :]
    sine_part = jnp.sin(angles)[:, None, :]
    leading = vectors[..., :half_dim]
    trailing = vectors[..., half_dim:]
    return jnp.concatenate(
        [leading * cosine - trailing * sine_part, trailing * cosine + leading * sine_part], axis=-1
    )


def layout_of(starts, lengths, buffer_len):
    token_index = jnp.arange(buffer_len, dtype=jnp.int32)
    inside = (token_index[:, None] >= starts[None, :]) & (
        token_index[:, None] < (starts + lengths)[None, :]
    )
    slot_number = jnp.arange(starts.shape[0], dtype=jnp.int32)
    segment = jnp.sum(jnp.where(inside, slot_number[None, :] + 1, 0), axis=1) - 1
    position = jnp.sum(jnp.where(inside, token_index[:, None] - starts[None, :], 0), axis=1)
    return (segment, position, inside)


def allowed_mask(segment, row_start, row_count, col_count):
    rows_index = row_start + jnp.arange(row_count, dtype=jnp.int32)
    cols_index = jnp.arange(col_count, dtype=jnp.int32)
    seg_rows = segment[row_start : row_start + row_count]
    seg_cols = segment[:col_count]
    same = (
        (seg_rows[:, None] == seg_cols[None, :])
        & (seg_rows[:, None] >= 0)
        & (cols_index[None, :] < rows_index[:, None])
    )
    return (rows_index[:, None] == cols_index[None, :]) | same


def softmax_rows(scores, permitted):
    masked_scores = jnp.where(permitted[None, None], scores, NEG_FILL)
    row_peak = jnp.max(masked_scores, axis=-1, keepdims=True)
    exponent = jnp.exp(masked_scores - row_peak)
    totals = jnp.sum(exponent, axis=-1, keepdims=True)
    return (exponent / totals).astype(jnp.bfloat16)


def pick_block(length_rows):
    for candidate in (512, 384, 256, 128):
        return candidate
    return length_rows


def per_device(
    tokens,
    norm_gain,
    w_query,
    w_key,
    w_value,
    w_out,
    seq_starts,
    seq_lengths,
    episode_ids,
    class_ids,
    query_flags,
):
    buffer_len = tokens.shape[0]
    model_width = tokens.shape[1]
    seq_count = seq_starts.shape[0]
    head_dim = HEAD_DIM
    heads_local = w_query.shape[1] // head_dim
    kv_local = w_key.shape[1] // head_dim
    group_size = heads_local // kv_local
    inv_root = 1.0 / math.sqrt(head_dim)
    highest = lax.Precision.HIGHEST
    segment, position, inside = layout_of(seq_starts, seq_lengths, buffer_len)
    widened = tokens.astype(jnp.float32)
    normed = (
        widened
        * lax.rsqrt(jnp.mean(widened * widened, axis=-1, keepdims=True) + 1e-05)
        * norm_gain.astype(jnp.float32)
    ).astype(jnp.bfloat16)
    queries = rotate(
        jnp.dot(normed, w_query, preferred_element_type=jnp.float32).reshape(
            buffer_len, heads_local, head_dim
        ),
        position,
    ).astype(jnp.bfloat16)
    queries = queries.reshape(buffer_len, kv_local, group_size, head_dim)
    keys_rot = rotate(
        jnp.dot(normed, w_key, preferred_element_type=jnp.float32).reshape(
            buffer_len, kv_local, head_dim
        ),
        position,
    ).astype(jnp.bfloat16)
    values_all = (
        jnp.dot(normed, w_value, preferred_element_type=jnp.float32)
        .astype(jnp.bfloat16)
        .reshape(buffer_len, kv_local, head_dim)
    )
    block_rows = pick_block(buffer_len)
    block_count = buffer_len // block_rows
    mixed_blocks = []
    for query_block in range(block_count):
        row_start = query_block * block_rows
        key_end = row_start + block_rows
        block_queries = queries[row_start:key_end]
        permitted = allowed_mask(segment, row_start, block_rows, key_end)
        scores = (
            jnp.einsum(
                "qngd,knd->ngqk",
                block_queries,
                keys_rot[:key_end],
                preferred_element_type=jnp.float32,
            )
            * inv_root
        )
        attention_probs = softmax_rows(scores, permitted)
        mixed_out = jnp.einsum(
            "ngqk,knd->qngd",
            attention_probs,
            values_all[:key_end],
            preferred_element_type=jnp.float32,
        )
        mixed_blocks.append(
            mixed_out.astype(jnp.bfloat16).reshape(block_rows, heads_local * head_dim)
        )
    attended = jnp.concatenate(mixed_blocks, axis=0)
    member = inside.T.astype(jnp.bfloat16)
    attended_sums = jnp.dot(member, attended, preferred_element_type=jnp.float32)
    token_sums = jnp.dot(member, tokens, preferred_element_type=jnp.float32)
    high_part = attended_sums.astype(jnp.bfloat16)
    low_part = (attended_sums - high_part.astype(jnp.float32)).astype(jnp.bfloat16)
    head_part = jnp.dot(high_part, w_out, preferred_element_type=jnp.float32) + jnp.dot(
        low_part, w_out, preferred_element_type=jnp.float32
    )
    token_counts = seq_lengths.astype(jnp.float32)[:, None]
    mp_size = lax.axis_size("mp")
    mp_rank = lax.axis_index("mp")
    share_cols = model_width // mp_size
    pooled = (token_sums + taken_together(head_part, "mp")) / token_counts
    embedded = pooled * lax.rsqrt(jnp.mean(pooled * pooled, axis=-1, keepdims=True) + 1e-06)
    seq_total = episode_ids.shape[0]
    episodes = max(1, seq_total // (2 * WAYS))
    classes = episodes * WAYS
    global_class = episode_ids * WAYS + class_ids
    is_support = query_flags == 0
    class_range = jnp.arange(classes, dtype=jnp.int32)
    select_all = ((global_class[None, :] == class_range[:, None]) & is_support[None, :]).astype(
        jnp.float32
    )
    dp_first = lax.axis_index("dp") * seq_count
    class_sums = jnp.dot(
        select_all, lax.all_gather(embedded, "dp", axis=0, tiled=True), precision=highest
    )
    proto_scale = jnp.mean(class_sums * class_sums, axis=-1)
    prototypes = class_sums * lax.rsqrt(proto_scale + 1e-06)[:, None]
    difference = embedded[:, None, :] - prototypes[None, :, :]
    distance = jnp.sum(difference * difference, axis=-1)
    proto_out = lax.dynamic_slice_in_dim(prototypes, mp_rank * share_cols, share_cols, 1)
    own_episode = lax.dynamic_slice_in_dim(episode_ids, dp_first, seq_count, 0)
    own_query = lax.dynamic_slice_in_dim(query_flags, dp_first, seq_count, 0)
    episode_range = jnp.arange(episodes, dtype=jnp.int32)
    picked = jnp.sum(
        jnp.where(
            own_episode[:, None, None] == episode_range[None, :, None],
            distance.reshape(seq_count, episodes, WAYS),
            0.0,
        ),
        axis=1,
    )
    logits = -picked / math.sqrt(model_width)
    row_peak = jnp.max(logits, axis=-1, keepdims=True)
    shifted = logits - row_peak
    log_probs = shifted - jnp.log(jnp.sum(jnp.exp(shifted), axis=-1, keepdims=True))
    log_probs = jnp.where(own_query[:, None] == 1, log_probs, 0.0)
    return (log_probs, proto_out)


def solution(mesh):
    placed = (
        P("dp", None),
        P(),
        P(None, "mp"),
        P(None, "mp"),
        P(None, "mp"),
        P("mp", None),
        P("dp"),
        P("dp"),
        P(),
        P(),
        P(),
    )
    return jax.shard_map(
        per_device,
        mesh=mesh,
        in_specs=placed,
        out_specs=(P("dp", None), P(None, "mp")),
        check_vma=False,
    )
```

profile of v0, /device:TPU:1, one launch (start us, length us, event | category | flops | bytes accessed | tf_op | source)
XLA Modules:
  0.0 170.8 jit_solution(10671157367950942480)
XLA Ops:
  8.9 7.1 %fusion = f32[1536]{0:T(1024)S(1)} fusion(bf16[1536,4096]{1,0:T(8,128)(2,1)} %param.11), kind=kLoop, calls=%fused_computation.2 | loop fusion | flops 18872832 | bytes 12589056 | tf_op jit(solution)/shard_map/reduce_sum | solution.py:104
  16.0 8.2 %fusion.2 = bf16[1536,4096]{1,0:T(8,128)(2,1)S(1)} fusion(bf16[1536,4096]{1,0:T(8,128)(2,1)} %param.11, f32[4096]{0:T(1024)S(1)} %convert_element_type.82, f32[1536]{0:T(1024)S(1)} %add_rsqrt_fusion), kind=kLoop, calls=%fused_computation.4 | loop fusion | flops 25165824 | bytes 25188352 | tf_op jit(solution)/shard_map/convert_element_type | solution.py:106
  24.2 3.4 %convolution_convert_fusion = bf16[1536,128]{1,0:T(8,128)(2,1)S(1)} fusion(bf16[1536,4096]{1,0:T(8,128)(2,1)S(1)} %fusion.2, bf16[4096,128]{1,0:T(8,128)(2,1)S(1)} %copy-done), kind=kOutput, calls=%fused_computation.35 | convolution fusion | flops 1610809344 | bytes 14024704 | tf_op jit(solution)/shard_map/dot_general | solution.py:121
  27.7 5.5 %convolution_bitcast_fusion = f32[1536,1,128]{0,2,1:T(8,128)S(1)} fusion(bf16[1536,4096]{1,0:T(8,128)(2,1)S(1)} %fusion.2, bf16[4096,128]{1,0:T(8,128)(2,1)} %param.14), kind=kOutput, calls=%fused_computation.34 | convolution fusion | flops 1610612736 | bytes 14417920 | tf_op jit(solution)/shard_map/dot_general | solution.py:115
  33.2 9.7 %fusion.88 = f32[1536,512]{0,1:T(8,128)} fusion(bf16[1536,4096]{1,0:T(8,128)(2,1)S(1)} %fusion.2, bf16[4096,512]{1,0:T(8,128)(2,1)} %param.13), kind=kOutput, calls=%fused_computation.144 | convolution fusion | flops 6442450944 | bytes 19922944 | tf_op jit(solution)/shard_map/dot_general | solution.py:108
  42.9 4.3 %multiply_cosine_fusion = (f32[1536,64]{1,0:T(8,128)}, f32[1536,64]{1,0:T(8,128)}) fusion(f32[64]{0:T(128)S(1)} %negate_power_fusion, f32[1536]{0:T(1024)S(1)} %convert_element_type.85), kind=kLoop, calls=%fused_computation.58 | loop fusion | flops 98304 | bytes 792832 | tf_op jit(solution)/shard_map/cos | solution.py:31
  47.2 1.6 fusion.51
  48.8 3.3 %fusion.85 = (f32[1536,4,64]{0,2,1:T(8,128)}, f32[1536,4,64]{0,2,1:T(8,128)S(1)}) fusion(f32[1536,4,128]{0,2,1:T(8,128)} %bitcast.120), kind=kLoop, calls=%fused_computation.141 | loop fusion | bytes 6291456 | tf_op jit(solution)/shard_map/slice | solution.py:34
  52.1 3.4 %copy.52 = f32[1536,4,64]{2,0,1:T(8,128)} copy(f32[1536,4,64]{0,2,1:T(8,128)} %get-tuple-element.6) | data formatting | bytes 3145728
  55.5 2.3 %copy.51 = f32[1536,4,64]{2,0,1:T(8,128)} copy(f32[1536,4,64]{0,2,1:T(8,128)S(1)} %get-tuple-element.7) | data formatting | bytes 3145728
  58.9 4.0 %subtract_convert_fusion = (bf16[1536,4,64]{2,0,1:T(8,128)(2,1)S(1)}, bf16[1536,4,64]{2,0,1:T(8,128)(2,1)S(1)}) fusion(f32[1536,4,64]{2,0,1:T(8,128)} %copy.52, f32[1536,4,64]{2,0,1:T(8,128)} %copy.51, f32[1536,64]{1,0:T(8,128)} %get-tuple-element.11, f32[1536,64]{1,0:T(8,128)} %get-tuple-element.10), kind=kLoop, calls=%fused_computation.31 | loop fusion | flops 3145728 | bytes 5505024 | tf_op jit(solution)/shard_map/convert.4
  64.1 2.0 %fusion.6 = (f32[4,512]{1,0:T(4,128)S(1)}, f32[1024,512,4]{1,0,2:T(8,128)S(1)}) fusion(pred[512,1024]{0,1:T(8,128)(4,1)S(1)} %fusion.18, bf16[1536,4,64]{2,0,1:T(8,128)(2,1)S(1)} %get-tuple-element.4, bf16[1536,4,64]{2,0,1:T(8,128)(2,1)S(1)} %get-tuple-element.5, bf16[1536,1,64]{0,2,1:T(8,128)(2,1)S(1)} %get-tuple-element.9, ...), kind=kOutput, calls=%fused_computation.15 | convolution fusion | flops 544733184 | bytes 10887168 | tf_op jit(solution)/shard_map/qngd,knd->ngqk/dot_general | solution.py:134
  67.1 1.5 fusion.30
  68.5 1.9 %fusion.5 = f32[4,512]{1,0:T(4,128)S(1)} fusion(f32[1024,512,4]{1,0,2:T(8,128)S(1)} %get-tuple-element.23, f32[4,512]{1,0:T(4,128)S(1)} %get-tuple-element.22, pred[512,1024]{0,1:T(8,128)(4,1)S(1)} %fusion.18), kind=kLoop, calls=%fused_computation.14 | loop fusion | flops 8386560 | bytes 8929280 | tf_op jit(solution)/shard_map/reduce_sum | solution.py:68
  70.4 2.7 %fusion.27 = bf16[128,4,512]{2,0,1:T(8,128)(2,1)S(1)} fusion(f32[4,512]{1,0:T(4,128)S(1)} %fusion.5, f32[4,512]{1,0:T(4,128)S(1)} %get-tuple-element.22, f32[1024,512,4]{1,0,2:T(8,128)S(1)} %get-tuple-element.23, pred[512,1024]{0,1:T(8,128)(4,1)S(1)} %fusion.18, bf16[1536,128]{1,0:T(8,128)(2,1)S(1)} %convolution_convert_fusion), kind=kOutput, calls=%fused_computation.54 | convolution fusion | flops 547618816 | bytes 9715712 | tf_op jit(solution)/shard_map/ngqk,knd->qngd/dot_general | solution.py:143
  73.1 1.7 fusion.14
  74.8 2.8 %fusion.4 = (f32[4,512]{1,0:T(4,128)S(1)}, f32[1536,512,4]{1,0,2:T(8,128)S(1)}) fusion(pred[512,1536]{0,1:T(8,128)(4,1)S(1)} %fusion.14, bf16[1536,4,64]{2,0,1:T(8,128)(2,1)S(1)} %get-tuple-element.5, bf16[1536,4,64]{2,0,1:T(8,128)(2,1)S(1)} %get-tuple-element.4, bf16[1536,64]{0,1:T(8,128)(2,1)S(1)} %bitcast.119, bf16[1536,64]{0,1:T(8,128)(2,1)S(1)} %bitcast.118), kind=kOutput, calls=%fused_computation.10 | convolution fusion | flops 816576512 | bytes 15343616 | tf_op jit(solution)/shard_map/qngd,knd->ngqk/dot_general | solution.py:134
  77.6 2.8 %fusion.3 = f32[4,512]{1,0:T(4,128)S(1)} fusion(f32[1536,512,4]{1,0,2:T(8,128)S(1)} %get-tuple-element.21, f32[4,512]{1,0:T(4,128)S(1)} %get-tuple-element.20, pred[512,1536]{0,1:T(8,128)(4,1)S(1)} %fusion.14), kind=kLoop, calls=%fused_computation.9 | loop fusion | flops 12580864 | bytes 13385728 | tf_op jit(solution)/shard_map/reduce_sum | solution.py:68
  80.4 3.9 %fusion.33 = bf16[128,4,512]{2,0,1:T(8,128)(2,1)S(1)} fusion(f32[4,512]{1,0:T(4,128)S(1)} %fusion.3, f32[4,512]{1,0:T(4,128)S(1)} %get-tuple-element.20, f32[1536,512,4]{1,0,2:T(8,128)S(1)} %get-tuple-element.21, pred[512,1536]{0,1:T(8,128)(4,1)S(1)} %fusion.14, bf16[1536,128]{1,0:T(8,128)(2,1)S(1)} %convolution_convert_fusion), kind=kOutput, calls=%fused_computation.56 | convolution fusion | flops 821297152 | bytes 14303232 | tf_op jit(solution)/shard_map/ngqk,knd->qngd/dot_general | solution.py:143
  86.2 14.5 %all_to_all.5 = f32[4,8,4096]{2,1,0:T(8,128)S(1)} all-to-all(f32[4,8,4096]{2,1,0:T(8,128)S(1)} %broadcast_in_dim.74), channel_id=1, replica_groups=mesh['dp'=32,'mp'=4] {'mp'}, dimensions={0} | all-to-all | bytes 1048576 | tf_op jit(solution)/shard_map/all_to_all | solution.py:18
  100.8 6.5 %multiply_reduce_fusion.2 = (f32[8]{0:T(128)S(1)}, f32[8,4096]{1,0:T(8,128)S(1)}) fusion(f32[8]{0:T(128)S(1)} %get-tuple-element.18, f32[8,4096]{1,0:T(8,128)S(1)} %reduce_sum.114, bf16[1536,4096]{1,0:T(8,128)(2,1)} %param.11, s32[8]{0:T(128)S(1)} %get-tuple-element.19, s32[8]{0:T(128)S(1)} %copy-done.6), kind=kOutput, calls=%fused_computation.94 | convolution fusion | flops 100831224 | bytes 12845184 | tf_op jit(solution)/shard_map/dot_general | solution.py:155
  108.3 46.9 %all-gather.2.cloned.1.call-done = f32[256,4096]{1,0:T(8,128)} async-done(((f32[8,4096]{1,0:T(8,128)}), f32[256,4096]{1,0:T(8,128)}) %all-gather.2.cloned.1.call-update) | async-done | bytes 4194320 | tf_op jit(solution)/shard_map/all_gather | solution.py:178
  155.2 4.3 %multiply_reduce_fusion.1 = (f32[128]{0:T(128)S(1)}, f32[128,4096]{1,0:T(8,128)S(1)}) fusion(f32[256,4096]{1,0:T(8,128)} %all-gather.2.cloned.1.call-done, s32[256]{0:T(256)S(1)} %multiply_add_fusion, pred[256]{0:T(512)(128)(4,1)S(1)} %broadcast_compare_fusion.3), kind=kOutput, calls=%fused_computation.38 | convolution fusion | flops 1611726720 | bytes 6293248 | tf_op jit(solution)/shard_map/dot_general | solution.py:177
  159.8 1.9 %multiply_reduce_fusion = f32[8,128]{1,0:T(8,128)S(1)} fusion(f32[128,4096]{1,0:T(8,128)S(1)} %broadcast_multiply_fusion, f32[8,4096]{1,0:T(8,128)S(1)} %copy-done.3), kind=kLoop, calls=%fused_computation.5 | loop fusion | flops 12581888 | bytes 2232320 | tf_op jit(solution)/shard_map/reduce_sum | solution.py:183
  (62 shorter events, 10.0 us)
Async XLA Ops:
  7.2 17.0 %copy-start = (bf16[4096,128]{1,0:T(8,128)(2,1)S(1)}, bf16[4096,128]{1,0:T(8,128)(2,1)}, u32[]{:S(2)}) copy-start(bf16[4096,128]{1,0:T(8,128)(2,1)} %param.15) | copy-start | bytes 3145732
  7.2 148.0 %all-gather.2.cloned.1.call-start = ((), (), s32[]{:S(2)}) async-start(), calls=%async_computation.1 | async-start | bytes 4325376 | tf_op jit(solution)/shard_map/all_gather | solution.py:178
  8.8 7.1 %copy-start.4 = (s32[1536]{0:T(1024)}, s32[1536]{0:T(1024)S(1)}, u32[]{:S(2)}) copy-start(s32[1536]{0:T(1024)S(1)} %broadcast_add_fusion) | copy-start | bytes 18436
  8.8 7.1 %copy-start.7 = (bf16[4096]{0:T(1024)(128)(2,1)S(1)}, bf16[4096]{0:T(1024)(128)(2,1)}, u32[]{:S(2)}) copy-start(bf16[4096]{0:T(1024)(128)(2,1)} %param.12) | copy-start | bytes 24580
  52.1 6.0 %slice-start = ((s32[1536]{0:T(1024)}), s32[1024]{0:T(1024)S(1)}, s32[]{:S(2)}) async-start(s32[1536]{0:T(1024)} %copy-done.4), calls=%async_computation.2 | async-start | bytes 8192 | tf_op jit(solution)/shard_map/slice | solution.py:55
  70.4 2.7 %copy-start.5 = (s32[1536]{0:T(1024)S(1)}, s32[1536]{0:T(1024)}, u32[]{:S(2)}) copy-start(s32[1536]{0:T(1024)} %copy-done.4) | copy-start | bytes 18436
  80.4 4.0 %copy-start.6 = (s32[8]{0:T(128)S(1)}, s32[8]{0:T(128)}, u32[]{:S(2)}) copy-start(s32[8]{0:T(128)} %param.17) | copy-start | bytes 100
  80.4 4.5 %copy-start.2 = (bf16[512,4096]{1,0:T(8,128)(2,1)S(1)}, bf16[512,4096]{1,0:T(8,128)(2,1)}, u32[]{:S(2)}) copy-start(bf16[512,4096]{1,0:T(8,128)(2,1)} %param.16) | copy-start | bytes 12582916
  100.8 7.3 %copy-start.9 = (s32[256]{0:T(256)S(1)}, s32[256]{0:T(256)}, u32[]{:S(2)}) copy-start(s32[256]{0:T(256)} %param.19) | copy-start | bytes 3076
  100.8 7.4 %copy-start.10 = (s32[256]{0:T(256)S(1)}, s32[256]{0:T(256)}, u32[]{:S(2)}) copy-start(s32[256]{0:T(256)} %param.21) | copy-start | bytes 3076
  100.8 7.5 %copy-start.8 = (s32[256]{0:T(256)S(1)}, s32[256]{0:T(256)}, u32[]{:S(2)}) copy-start(s32[256]{0:T(256)} %param.20) | copy-start | bytes 3076
  108.3 51.5 %copy-start.3 = (f32[8,4096]{1,0:T(8,128)S(1)}, f32[8,4096]{1,0:T(8,128)}, u32[]{:S(2)}) copy-start(f32[8,4096]{1,0:T(8,128)} %broadcast_multiply_fusion.1) | copy-start | bytes 393220
  155.2 8.6 %copy-start.1 = (bf16[4096,128]{1,0:T(8,128)(2,1)S(1)}, bf16[4096,128]{1,0:T(8,128)(2,1)}, u32[]{:S(2)}) copy-start(bf16[4096,128]{1,0:T(8,128)(2,1)} %param.15) | copy-start | bytes 3145732
Sparse Core Ops, SparseCore 0:
  108.2 46.9 all-gather.1
where the time goes:
time: 174 us; the launch traced here: 171 us
  waiting for transfers between devices  46.9 us (27%)
  matrix products  45.4 us (26%)
  other arithmetic  39.2 us (23%)
  between operations  14.7 us (8%)
  blocking collectives  14.5 us (8%)
  local copies, waits for them, and re-layouts  10.1 us (6%)
    all_gather x1, waiting for transfers between devices, per_device(): lax.all_gather(embedded, 'dp', axis=0, tiled=True)  46.9 us
    all_to_all x1, blocking collectives, sent_to_all(): return lax.all_to_all(copies, axis, split_axis=0, concat_axis=0, tiled=True)  14.5 us
    dot_general x1, matrix products, per_device(): jnp.dot(normed, w_query, preferred_element_type=jnp.float32)  9.66 us
    convert_element_type x1, other arithmetic, per_device(): normed = (widened * lax.rsqrt(jnp.mean(widened * widened, axis=-1, keepdi...  8.22 us
    dot_general x3, matrix products, per_device(): jnp.einsum('ngqk,knd->qngd', attention_probs, values_all[:key_end], prefe...  8.09 us
    reduce_sum x1, other arithmetic, per_device(): jnp.mean(widened * widened, axis=-1, keepdims=True) + 1e-05  7.07 us
    dot_general x1, matrix products, per_device(): token_sums = jnp.dot(member, tokens, preferred_element_type=jnp.float32)  6.47 us
    dot_general x3, matrix products, per_device(): jnp.einsum('qngd,knd->ngqk', block_queries, keys_rot[:key_end], preferred...  6 us
  transfers between devices with their start and end apart: 1, of which 1 were waited for; matrix products, arithmetic and copies ran while one was open for 0% of the time, Pallas kernels for 0%

commit v1 on v0

v1 whole, which is shorter than its diff:
```python
import functools
import math

import jax
import jax.numpy as jnp
import numpy as np
from jax import lax
from jax.experimental import pallas as pl
from jax.experimental.pallas import tpu as pltpu
from jax.sharding import PartitionSpec as P

HEAD_DIM = 128
WAYS = 32
ROPE_BASE = 500000.0
LONGEST = 640
STEPS = 8
TILE = 128
ONES = 16
FAR = -(2.0**100)
F32 = jnp.float32
BF16 = jnp.bfloat16


def rope_tables(rows, block):
    half = HEAD_DIM // 2
    frequency = ROPE_BASE ** (-(np.arange(half, dtype=np.float64) * 2.0 / HEAD_DIM))
    frequency = np.concatenate([frequency, frequency])[None, :]
    sign = np.where(np.arange(HEAD_DIM) < half, -1.0, 1.0)[None, :]
    fine = np.arange(block, dtype=np.float64)[:, None] * frequency
    coarse = np.arange(0, rows, block, dtype=np.float64)[:, None] * frequency
    fine_table = np.stack([np.cos(fine), np.sin(fine)])
    coarse_table = np.stack(
        [np.cos(coarse), np.sin(coarse), sign * np.cos(coarse), sign * np.sin(coarse)]
    )
    return fine_table.astype(np.float32), coarse_table.astype(np.float32)


def dot(a, b):
    return jnp.dot(a, b, preferred_element_type=F32)


def dot_nt(a, b):
    return lax.dot_general(a, b, (((1,), (1,)), ((), ())), preferred_element_type=F32)


def local_kernel(
    starts,
    lengths,
    gain,
    fine,
    coarse,
    x_ref,
    wq_ref,
    wk_ref,
    wv_ref,
    att_ref,
    tok_ref,
    acc,
    squares,
    member,
    qs,
    ks,
    vt,
    ot,
):
    step = pl.program_id(0)
    rows, depth = x_ref.shape
    slots = starts.shape[0]
    heads = wq_ref.shape[1] // HEAD_DIM
    width = depth * STEPS
    tiles = rows // TILE
    half_rows = rows // 3

    @pl.when(step == 0)
    def _():
        token = lax.broadcasted_iota(jnp.int32, (ONES, rows), 1)
        slot = lax.broadcasted_iota(jnp.int32, (ONES, rows), 0)
        first = jnp.zeros((ONES, rows), jnp.int32)
        last = jnp.zeros((ONES, rows), jnp.int32)
        for s in range(slots):
            first = jnp.where(slot == s, starts[s], first)
            last = jnp.where(slot == s, starts[s] + lengths[s], last)
        member[...] = jnp.where((token >= first) & (token < last), 1.0, 0.0).astype(BF16)

    weights = jnp.concatenate([wq_ref[...], wk_ref[...], wv_ref[...]], axis=1)

    def project(fresh):
        for r in range(3):
            at = pl.ds(r * half_rows, half_rows)
            x = x_ref[at, :]
            wide = x.astype(F32)
            wide = wide * wide
            total = wide[:, 0:128]
            for c in range(1, depth // 128):
                total += wide[:, c * 128 : (c + 1) * 128]
            part = dot(x * gain[...], weights)
            if fresh:
                squares[at, :] = total
                acc[at, :] = part
            else:
                squares[at, :] += total
                acc[at, :] += part

    @pl.when(step == 0)
    def _():
        project(True)

    @pl.when(step > 0)
    def _():
        project(False)

    per_rank = STEPS // lax.axis_size("mp")
    rank = lax.axis_index("mp")

    for c in range(per_rank):

        @pl.when(step == rank * per_rank + c)
        def _():
            tok_ref[:, c * depth : (c + 1) * depth] = dot(member[...], x_ref[...])[:slots]

    @pl.when(step == STEPS - 1)
    def _():
        scale = math.log2(math.e) / math.sqrt(HEAD_DIM)
        lane = lax.broadcasted_iota(jnp.int32, (1, 128), 1)
        first = jnp.full((1, 128), rows, jnp.int32)
        last = jnp.full((1, 128), 0, jnp.int32)
        for s in range(slots):
            first = jnp.where(lane == s, starts[s], first)
            last = jnp.where(lane == s, starts[s] + lengths[s], last)
        fine_cos, fine_sin = fine[0], fine[1]
        for i in range(tiles):
            for h in range(TILE // 64):
                low = i * TILE + h * 64
                at = pl.ds(low, 64)
                row_scale = lax.rsqrt(
                    jnp.sum(squares[at, :], axis=1, keepdims=True) * (1.0 / width) + 1e-05
                )
                block = low // 64
                cos_a, sin_a = coarse[0, block : block + 1, :], coarse[1, block : block + 1, :]
                cos_s, sin_s = coarse[2, block : block + 1, :], coarse[3, block : block + 1, :]
                cosine = (cos_a * fine_cos - sin_a * fine_sin) * row_scale
                sine = (sin_s * fine_cos + cos_s * fine_sin) * row_scale
                token = low + lax.broadcasted_iota(jnp.int32, (64, 128), 0)
                inside = (token >= first) & (token < last)
                q_mark = jnp.where(inside, 1.0, 0.0).astype(BF16)
                k_mark = jnp.where(inside, 0.0, FAR).astype(BF16)
                for n in range(heads):
                    v = acc[at, n * 128 : (n + 1) * 128]
                    v = v * cosine + pltpu.roll(v, 64, 1) * sine
                    to = pl.ds(n * TILE + h * 64, 64)
                    qs[i, to, 0:128] = v.astype(BF16)
                    qs[i, to, 128:256] = q_mark
                v = acc[at, heads * 128 : (heads + 1) * 128] * scale
                v = v * cosine + pltpu.roll(v, 64, 1) * sine
                ks[at, 0:128] = v.astype(BF16)
                ks[at, 128:256] = k_mark
            at = pl.ds(i * TILE, TILE)
            row_scale = lax.rsqrt(
                jnp.sum(squares[at, :], axis=1, keepdims=True) * (1.0 / width) + 1e-05
            )
            v = acc[at, (heads + 1) * 128 : (heads + 2) * 128] * row_scale
            vt[0:128, at] = v.T.astype(BF16)
            vt[128 : 128 + ONES, at] = jnp.ones((ONES, TILE), BF16)
        key = lax.broadcasted_iota(jnp.int32, (TILE, heads * TILE), 0)
        query = lax.broadcasted_iota(jnp.int32, (TILE, heads * TILE), 1) % TILE
        causal = key <= query
        for i in range(tiles):
            begin = max(0, i * TILE - LONGEST)
            count = (i * TILE - begin) // TILE
            scores = []
            for c in range(count + 1):
                s = dot_nt(ks[begin + c * TILE : begin + (c + 1) * TILE, :], qs[i])
                if c == count:
                    s = jnp.where(causal, s, FAR)
                scores.append(s)
            s = jnp.concatenate(scores, axis=0)
            e = jnp.exp2(s - jnp.max(s, axis=0, keepdims=True)).astype(BF16)
            o = dot(vt[:, begin : (i + 1) * TILE], e)
            o = (o[0:128] / o[128:129]).astype(BF16)
            for n in range(heads):
                ot[n * 128 : (n + 1) * 128, i * TILE : (i + 1) * TILE] = o[
                    :, n * TILE : (n + 1) * TILE
                ]
        att_ref[...] = dot_nt(member[...], ot[...])[:slots]


def local_part(tokens, norm_gain, w_query, w_key, w_value, seq_starts, seq_lengths):
    rows, width = tokens.shape
    slots = seq_starts.shape[0]
    heads = w_query.shape[1] // HEAD_DIM
    columns = w_query.shape[1] + w_key.shape[1] + w_value.shape[1]
    depth = width // STEPS
    fine, coarse = rope_tables(rows, 64)
    share = width // lax.axis_size("mp")
    tiles = rows // TILE
    whole = lambda shape: pl.BlockSpec(shape, lambda k: (0,) * len(shape))
    return pl.pallas_call(
        local_kernel,
        grid=(STEPS,),
        out_shape=(
            jax.ShapeDtypeStruct((slots, heads * HEAD_DIM), F32),
            jax.ShapeDtypeStruct((slots, share), F32),
        ),
        in_specs=[
            pl.BlockSpec(memory_space=pltpu.SMEM),
            pl.BlockSpec(memory_space=pltpu.SMEM),
            pl.BlockSpec((1, depth), lambda k: (0, k)),
            whole(fine.shape),
            whole(coarse.shape),
            pl.BlockSpec((rows, depth), lambda k: (0, k)),
            pl.BlockSpec((depth, w_query.shape[1]), lambda k: (k, 0)),
            pl.BlockSpec((depth, w_key.shape[1]), lambda k: (k, 0)),
            pl.BlockSpec((depth, w_value.shape[1]), lambda k: (k, 0)),
        ],
        out_specs=(whole((slots, heads * HEAD_DIM)), whole((slots, share))),
        scratch_shapes=[
            pltpu.VMEM((rows, columns), F32),
            pltpu.VMEM((rows, 128), F32),
            pltpu.VMEM((ONES, rows), BF16),
            pltpu.VMEM((tiles, heads * TILE, 256), BF16),
            pltpu.VMEM((rows, 256), BF16),
            pltpu.VMEM((128 + ONES, rows), BF16),
            pltpu.VMEM((heads * HEAD_DIM, rows), BF16),
        ],
        compiler_params=pltpu.CompilerParams(
            dimension_semantics=("arbitrary",), vmem_limit_bytes=44 * 2**20
        ),
        name="local_part",
    )(
        seq_starts,
        seq_lengths,
        norm_gain.reshape(1, width),
        jnp.asarray(fine),
        jnp.asarray(coarse),
        tokens,
        w_query,
        w_key,
        w_value,
    )


def per_device(
    tokens,
    norm_gain,
    w_query,
    w_key,
    w_value,
    w_out,
    seq_starts,
    seq_lengths,
    episode_ids,
    class_ids,
    query_flags,
):
    width = tokens.shape[1]
    slots = seq_starts.shape[0]
    attended, token_sums = local_part(
        tokens, norm_gain, w_query, w_key, w_value, seq_starts, seq_lengths
    )
    high = attended.astype(BF16)
    low = (attended - high.astype(F32)).astype(BF16)
    both = dot(jnp.concatenate([high, low], axis=0), w_out)
    head_part = both[:slots] + both[slots:]
    mp = lax.axis_size("mp")
    share = width // mp
    pieces = head_part.reshape(slots, mp, share).transpose(1, 0, 2)
    pieces = lax.all_to_all(pieces, "mp", split_axis=0, concat_axis=0, tiled=True)
    pooled = (token_sums + pieces.sum(axis=0)) / seq_lengths.astype(F32)[:, None]
    square = lax.psum(jnp.sum(pooled * pooled, axis=-1, keepdims=True), "mp")
    embedded = pooled * lax.rsqrt(square / width + 1e-06)
    everyone = lax.all_gather(embedded, "dp", axis=0, tiled=True)
    seq_total = episode_ids.shape[0]
    episodes = max(1, seq_total // (2 * WAYS))
    classes = episodes * WAYS
    global_class = episode_ids * WAYS + class_ids
    class_range = jnp.arange(classes, dtype=jnp.int32)
    select = (
        (global_class[None, :] == class_range[:, None]) & (query_flags == 0)[None, :]
    ).astype(F32)
    highest = lax.Precision.HIGHEST
    sums = jnp.dot(select, everyone, precision=highest)
    cross = lax.dot_general(embedded, sums, (((1,), (1,)), ((), ())), precision=highest)
    packed = jnp.concatenate([cross, jnp.sum(sums * sums, axis=1)[None, :]], axis=0)
    packed = lax.psum(packed, "mp")
    mean_square = packed[slots] / width
    scale = lax.rsqrt(mean_square + 1e-06)
    prototypes = sums * scale[:, None]
    own_square = (square / width) / (square / width + 1e-06) * width
    distance = (
        own_square - 2.0 * packed[:slots] * scale[None, :] + (mean_square * scale * scale * width)[None, :]
    )
    own_first = lax.axis_index("dp") * slots
    own_episode = lax.dynamic_slice_in_dim(episode_ids, own_first, slots, 0)
    own_query = lax.dynamic_slice_in_dim(query_flags, own_first, slots, 0)
    picked = jnp.sum(
        jnp.where(
            own_episode[:, None, None] == jnp.arange(episodes, dtype=jnp.int32)[None, :, None],
            distance.reshape(slots, episodes, WAYS),
            0.0,
        ),
        axis=1,
    )
    logits = -picked / math.sqrt(width)
    shifted = logits - jnp.max(logits, axis=-1, keepdims=True)
    log_probs = shifted - jnp.log(jnp.sum(jnp.exp(shifted), axis=-1, keepdims=True))
    return jnp.where(own_query[:, None] == 1, log_probs, 0.0), prototypes


def solution(mesh):
    placed = (
        P("dp", None),
        P(),
        P(None, "mp"),
        P(None, "mp"),
        P(None, "mp"),
        P("mp", None),
        P("dp"),
        P("dp"),
        P(),
        P(),
        P(),
    )
    return jax.shard_map(
        per_device,
        mesh=mesh,
        in_specs=placed,
        out_specs=(P("dp", None), P(None, "mp")),
        check_vma=False,
    )
```

time: 174 us -> 127 us (0.73)
  matrix products: 45.4 us -> 3.74 us
  other arithmetic: 39.2 us -> 3.81 us
  Pallas kernels: 0 us -> 23.6 us
  starting transfers between devices: 0.04 us -> 5.86 us
  waiting for transfers between devices: 46.9 us -> 50.2 us
    dot_general x14 -> x3, matrix products: 45.4 us -> 3.74 us  [the longest x1 1.82 us: per_device(): sums = jnp.dot(select, everyone, precision=highest)]
    pallas_call x0 -> x1, Pallas kernels: none -> 23.6 us  [local_part(): pl.pallas_call(local_kernel, grid=(STEPS,), out_shape=(jax.ShapeDtypeStru...]
    psum x0 -> x2, blocking collectives: none -> 15.7 us  [the longest x1 8.78 us: per_device(): packed = lax.psum(packed, 'mp')]
    reduce_sum x8 -> x3, other arithmetic: 15.4 us -> 0.29 us  [the longest x1 0.19 us: per_device(): square = lax.psum(jnp.sum(pooled * pooled, axis=-1, keepdims=True), 'mp')]
    all_to_all x1 -> x0, blocking collectives: 14.5 us -> none  [sent_to_all(): return lax.all_to_all(copies, axis, split_axis=0, concat_axis=0, tiled=True)]
    convert_element_type x4 -> x2, other arithmetic: 9 us -> 0.01 us  [the longest x1 0.01 us: per_device(): low = (attended - high.astype(F32)).astype(BF16)]
    all_to_all x0 -> x1, starting transfers between devices: none -> 5.86 us  [per_device(): lax.all_to_all(pieces, 'mp', split_axis=0, concat_axis=0, tiled=True)]
    another operation x2 -> x0, other arithmetic: 5.66 us -> none
  transfers between devices with their start and end apart: 1 -> 2, of which waited for: 1 -> 2; matrix products, arithmetic and copies ran while one was open for 0% -> 0% of each run, Pallas kernels for 0% -> 0%
where the time goes in v1:
time: 127 us; the launch traced here: 125 us
  waiting for transfers between devices  50.2 us (40%)
  Pallas kernels  23.6 us (19%)
  blocking collectives  15.7 us (12%)
  between operations  14.1 us (11%)
  local copies, waits for them, and re-layouts  8.49 us (7%)
  starting transfers between devices  5.86 us (5%)
  other arithmetic  3.81 us (3%)
  matrix products  3.74 us (3%)
    all_gather x1, waiting for transfers between devices, per_device(): everyone = lax.all_gather(embedded, 'dp', axis=0, tiled=True)  45.4 us
    pallas_call x1, Pallas kernels, local_part(): pl.pallas_call(local_kernel, grid=(STEPS,), out_shape=(jax.ShapeDtypeStru...  23.6 us
    psum x1, blocking collectives, per_device(): packed = lax.psum(packed, 'mp')  8.78 us
    unnamed x24, local copies, waits for them, and re-layouts  7.62 us
    psum x1, blocking collectives, per_device(): square = lax.psum(jnp.sum(pooled * pooled, axis=-1, keepdims=True), 'mp')  6.88 us
    all_to_all x1, starting transfers between devices, per_device(): lax.all_to_all(pieces, 'mp', split_axis=0, concat_axis=0, tiled=True)  5.86 us
    all_to_all x1, waiting for transfers between devices, per_device(): lax.all_to_all(pieces, 'mp', split_axis=0, concat_axis=0, tiled=True)  4.82 us
  transfers between devices with their start and end apart: 2, of which 2 were waited for; matrix products, arithmetic and copies ran while one was open for 0% of the time, Pallas kernels for 0%

profile of v1, /device:TPU:1, one launch (start us, length us, event | category | flops | bytes accessed | tf_op | source)
XLA Modules:
  0.0 125.4 jit_solution(9633169743154640670)
XLA Ops:
  7.2 0.7 reshape.62.gain
  7.9 2.2 %copy-done = bf16[4096,512]{1,0:T(8,128)(2,1)S(1)} copy-done((bf16[4096,512]{1,0:T(8,128)(2,1)S(1)}, bf16[4096,512]{1,0:T(8,128)(2,1)}, u32[]{:S(2)}) %copy-start) | copy-done | bytes 4194328
  10.1 1.2 copy-done.1
  11.3 1.2 copy-done.2
  12.5 0.8 copy-done.3
  13.4 0.8 copy-done.4
  14.2 0.7 copy-done.5
  14.8 0.7 copy-done.6
  15.5 23.6 %local_part.1 = (f32[8,512]{1,0:T(8,128)S(1)}, f32[8,1024]{1,0:T(8,128)S(1)}) custom-call(s32[8]{0:T(128)S(1)} %copy-done.5, s32[8]{0:T(128)S(1)} %copy-done.6, bf16[1,4096]{1,0:T(2,128)(2,1)S(1)} %reshape.62.gain, f32[2,64,128]{2,1,0:T(8,128)S(1)} %copy-done.3, f32[4,24,128]{2,1,0:T(8,128)S(1)} %copy-done.4, bf16[1536,4096]{1,0:T(8,128)(2,1)} %x_ref.1, ...), custom_call_target="tpu_custom_call" | custom-call | tf_op jit(solution)/shard_map/local_part/pallas_call | solution.py:197
  39.1 0.7 fusion.5
  39.8 0.7 slice_add_fusion
  40.4 5.9 %all-to-all-start = ((f32[4,8,1024]{2,1,0:T(8,128)}), f32[4,8,1024]{2,1,0:T(8,128)S(1)}, u32[]{:S(2)}, u32[]{:S(2)}) async-start(f32[4,8,1024]{2,1,0:T(8,128)} %bitcast.1), calls=%async_computation | async-start | bytes 262144 | tf_op jit(solution)/shard_map/all_to_all | solution.py:267
  46.3 4.8 %all-to-all-done = f32[4,8,1024]{2,1,0:T(8,128)S(1)} async-done(((f32[4,8,1024]{2,1,0:T(8,128)}), f32[4,8,1024]{2,1,0:T(8,128)S(1)}, u32[]{:S(2)}, u32[]{:S(2)}) %all-to-all-start) | async-done | bytes 131104 | tf_op jit(solution)/shard_map/all_to_all | solution.py:267
  51.1 0.2 multiply_reduce_fusion.1
  51.3 6.9 %psum.14 = f32[8,1]{0,1:T(1,128)S(1)} all-reduce(f32[8,1]{0,1:T(1,128)S(1)} %bitcast.20), channel_id=1, replica_groups=mesh['dp'=32,'mp'=4] {'mp'}, use_global_device_ids=true, to_apply=%region_2.0 | all-reduce | flops 8 | bytes 64 | tf_op jit(solution)/shard_map/psum | solution.py:269
  58.2 0.7 broadcast_multiply_fusion.1
  59.2 45.4 %all-gather.2.cloned.1.call-done = f32[256,1024]{1,0:T(8,128)} async-done(((f32[8,1024]{1,0:T(8,128)}), f32[256,1024]{1,0:T(8,128)}) %all-gather.2.cloned.1.call-update) | async-done | bytes 1048592 | tf_op jit(solution)/shard_map/all_gather | solution.py:271
  104.6 1.8 %multiply_reduce_fusion = (f32[128]{0:T(128)S(1)}, f32[128,1024]{1,0:T(8,128)S(1)}) fusion(f32[256,1024]{1,0:T(8,128)} %all-gather.2.cloned.1.call-done, s32[256]{0:T(256)S(1)} %multiply_add_fusion, pred[256]{0:T(512)(128)(4,1)S(1)} %broadcast_compare_fusion), kind=kOutput, calls=%fused_computation | convolution fusion | flops 402980736 | bytes 1574656 | tf_op jit(solution)/shard_map/dot_general | solution.py:281
  106.4 1.3 %fusion.19 = f32[8,128]{1,0:T(8,128)S(1)} fusion(f32[8,1024]{1,0:T(8,128)} %broadcast_multiply_fusion.1, f32[128,1024]{1,0:T(8,128)S(1)} %get-tuple-element.14), kind=kOutput, calls=%fused_computation.42 | convolution fusion | flops 12582912 | bytes 561152 | tf_op jit(solution)/shard_map/dot_general | solution.py:282
  107.7 8.8 %psum.15 = f32[9,128]{1,0:T(8,128)S(1)} all-reduce(f32[9,128]{1,0:T(8,128)S(1)} %pad_maximum_fusion), channel_id=1, replica_groups=mesh['dp'=32,'mp'=4] {'mp'}, use_global_device_ids=true, to_apply=%region_4.0 | all-reduce | flops 1152 | bytes 9216 | tf_op jit(solution)/shard_map/psum | solution.py:284
  116.5 0.9 broadcast_multiply_fusion
  117.6 0.1 fusion.11
  117.7 0.2 exponential_reduce_fusion
  117.9 0.7 subtract_select_fusion
  (34 shorter events, 0.6 us)
Async XLA Ops:
  7.9 2.2 %copy-start = (bf16[4096,512]{1,0:T(8,128)(2,1)S(1)}, bf16[4096,512]{1,0:T(8,128)(2,1)}, u32[]{:S(2)}) copy-start(bf16[4096,512]{1,0:T(8,128)(2,1)} %wq_ref.1) | copy-start | bytes 12582916
  10.1 1.2 copy-start.1
  11.3 1.2 copy-start.2
  12.5 0.8 copy-start.3
  13.4 0.8 copy-start.4
  14.2 0.7 copy-start.5
  14.8 0.7 copy-start.6
  15.5 23.6 %copy-start.8 = (bf16[512,4096]{1,0:T(8,128)(2,1)S(1)}, bf16[512,4096]{1,0:T(8,128)(2,1)}, u32[]{:S(2)}) copy-start(bf16[512,4096]{1,0:T(8,128)(2,1)} %param.18) | copy-start | bytes 12582916
  39.0 7.3 %copy-start.7 = (s32[8]{0:T(128)S(1)}, s32[8]{0:T(128)}, u32[]{:S(2)}) copy-start(s32[8]{0:T(128)} %lengths.1) | copy-start | bytes 100
  39.0 19.9 %copy-start.10 = (s32[256]{0:T(256)S(1)}, s32[256]{0:T(256)}, u32[]{:S(2)}) copy-start(s32[256]{0:T(256)} %param.21) | copy-start | bytes 3076
  39.0 20.0 %copy-start.11 = (s32[256]{0:T(256)S(1)}, s32[256]{0:T(256)}, u32[]{:S(2)}) copy-start(s32[256]{0:T(256)} %param.23) | copy-start | bytes 3076
  39.1 20.1 %copy-start.9 = (s32[256]{0:T(256)S(1)}, s32[256]{0:T(256)}, u32[]{:S(2)}) copy-start(s32[256]{0:T(256)} %param.22) | copy-start | bytes 3076
  40.4 10.7 %all-to-all-start = ((f32[4,8,1024]{2,1,0:T(8,128)}), f32[4,8,1024]{2,1,0:T(8,128)S(1)}, u32[]{:S(2)}, u32[]{:S(2)}) async-start(f32[4,8,1024]{2,1,0:T(8,128)} %bitcast.1), calls=%async_computation | async-start | bytes 262144 | tf_op jit(solution)/shard_map/all_to_all | solution.py:267
  46.3 58.3 %all-gather.2.cloned.1.call-start = ((), (), s32[]{:S(2)}) async-start(), calls=%async_computation.1 | async-start | bytes 1081344 | tf_op jit(solution)/shard_map/all_gather | solution.py:271
Sparse Core Ops, SparseCore 0:
  59.1 45.4 all-gather.1

commit v2 on v1

--- a/solution.py
+++ b/solution.py
@@ -239,6 +239,318 @@
     )
 
 
+def split(a):
+    high = a.astype(BF16)
+    return high, (a - high.astype(F32)).astype(BF16)
+
+
+def exchange_kernel(
+    lengths,
+    episode_s,
+    flag_s,
+    episode_v,
+    class_v,
+    flag_v,
+    att_ref,
+    tok_ref,
+    wo_ref,
+    log_ref,
+    proto_ref,
+    part,
+    landed,
+    everyone,
+    square_part,
+    square_landed,
+    squares,
+    final_part,
+    final_landed,
+    rs_send,
+    rs_recv,
+    sq_send,
+    sq_recv,
+    ag_send,
+    ag_recv,
+    relay_send,
+    relay_recv,
+    all_send,
+    all_recv,
+    fin_send,
+    fin_recv,
+):
+    mp = lax.axis_size("mp")
+    dp = lax.axis_size("dp")
+    me = lax.axis_index("mp")
+    mine = lax.axis_index("dp")
+    slots = att_ref.shape[0]
+    share = tok_ref.shape[1]
+    width = share * mp
+    side = int(math.isqrt(dp // 2))
+    x, y, core = mine // (2 * side), (mine // 2) % side, mine % 2
+    partner = mine + 1 - 2 * core
+
+    def at(dx, dy):
+        return (((x + dx + side) % side) * side + (y + dy + side) % side) * 2 + core
+
+    barrier = pltpu.get_barrier_semaphore()
+    for d in range(1, mp):
+        pl.semaphore_signal(barrier, inc=1, device_id={"mp": (me + d) % mp})
+
+    def greet(d, carry):
+        pl.semaphore_signal(barrier, inc=1, device_id={"dp": (mine + d) % dp})
+        return carry
+
+    lax.fori_loop(1, dp, greet, 0)
+
+    high, low = split(att_ref[...])
+    stacked = jnp.concatenate([high, low], axis=0)
+    for r in range(mp):
+        both = dot(stacked, wo_ref[:, r * share : (r + 1) * share])
+        part[r] = both[:slots] + both[slots:]
+
+    pl.semaphore_wait(barrier, mp - 1 + dp - 1)
+
+    order = sorted(range(1, mp), key=lambda d: -min(d, mp - d))
+    copies = {}
+    for d in order:
+        copies[d] = pltpu.make_async_remote_copy(
+            src_ref=part.at[(me + d) % mp],
+            dst_ref=landed.at[d - 1],
+            send_sem=rs_send.at[d - 1],
+            recv_sem=rs_recv.at[d - 1],
+            device_id={"mp": (me + d) % mp},
+        )
+        copies[d].start()
+    row = lax.broadcasted_iota(jnp.int32, (slots, 1), 0)
+    count = jnp.ones((slots, 1), jnp.int32)
+    for s in range(slots):
+        count = jnp.where(row == s, lengths[s], count)
+    pooled = tok_ref[...] + part[me]
+    for d in reversed(order):
+        copies[d].wait_recv()
+        pooled += landed[d - 1]
+    pooled = pooled / count.astype(F32)
+    everyone[mine] = pooled
+
+    offsets = [(dx, dy) for dx in range(side) for dy in range(side) if dx or dy]
+    reach = lambda o: min(o[0], side - o[0]) + min(o[1], side - o[1])
+    offsets = sorted(offsets, key=lambda o: -reach(o))
+    sends = []
+    for i, (dx, dy) in enumerate(offsets):
+        copy = pltpu.make_async_remote_copy(
+            src_ref=everyone.at[mine],
+            dst_ref=everyone.at[mine],
+            send_sem=ag_send.at[i],
+            recv_sem=ag_recv.at[i],
+            device_id={"dp": at(dx, dy)},
+        )
+        copy.start()
+        sends.append(copy)
+    relays = [
+        pltpu.make_async_remote_copy(
+            src_ref=everyone.at[mine],
+            dst_ref=everyone.at[mine],
+            send_sem=relay_send.at[len(offsets)],
+            recv_sem=relay_recv.at[len(offsets)],
+            device_id={"dp": partner},
+        )
+    ]
+    relays[0].start()
+
+    lane = lax.broadcasted_iota(jnp.int32, (slots, 128), 1)
+    slot = lax.broadcasted_iota(jnp.int32, (slots, 128), 0)
+    square = jnp.sum(pooled * pooled, axis=1, keepdims=True)
+    square = jnp.sum(jnp.where(lane == slot, square, 0.0), axis=0, keepdims=True)
+    square_part[...] = square
+    copies_sq = {}
+    for d in order:
+        copies_sq[d] = pltpu.make_async_remote_copy(
+            src_ref=square_part,
+            dst_ref=square_landed.at[d - 1],
+            send_sem=sq_send.at[d - 1],
+            recv_sem=sq_recv.at[d - 1],
+            device_id={"mp": (me + d) % mp},
+        )
+        copies_sq[d].start()
+    for d in reversed(order):
+        copies_sq[d].wait_recv()
+        square += square_landed[d - 1]
+    squares[mine] = square
+
+    def share_square(d):
+        return pltpu.make_async_remote_copy(
+            src_ref=squares.at[mine],
+            dst_ref=squares.at[mine],
+            send_sem=all_send.at[d - 1],
+            recv_sem=all_recv.at[d - 1],
+            device_id={"dp": (mine + d) % dp},
+        )
+
+    def start_square(d, carry):
+        share_square(d).start()
+        return carry
+
+    lax.fori_loop(1, dp, start_square, 0)
+
+    for i in reversed(range(len(offsets))):
+        dx, dy = offsets[i]
+        sends[i].wait_recv()
+        source = at(-dx, -dy)
+        copy = pltpu.make_async_remote_copy(
+            src_ref=everyone.at[source],
+            dst_ref=everyone.at[source],
+            send_sem=relay_send.at[i],
+            recv_sem=relay_recv.at[i],
+            device_id={"dp": partner},
+        )
+        copy.start()
+        relays.append(copy)
+
+    total = dp * slots
+    classes = proto_ref.shape[0]
+    named = episode_v[...] * WAYS + class_v[...]
+    named = jnp.where(flag_v[...] == 0, named, -1).reshape(1, total)
+    kind = lax.broadcasted_iota(jnp.int32, (classes, total), 0)
+    select = jnp.where(kind == named, 1.0, 0.0).astype(BF16)
+
+    def wait_square(d, carry):
+        share_square(d).wait_recv()
+        return carry
+
+    lax.fori_loop(1, dp, wait_square, 0)
+    spread = jnp.where(
+        lax.broadcasted_iota(jnp.int32, (dp, slots, 128), 2)
+        == lax.broadcasted_iota(jnp.int32, (dp, slots, 128), 1),
+        squares[...],
+        0.0,
+    )
+    mean = jnp.sum(spread, axis=2, keepdims=True) * (1.0 / width)
+    weight = lax.rsqrt(mean + 1e-06)
+    for copy in relays:
+        copy.wait_recv()
+    scaled = (everyone[...] * weight).reshape(total, share)
+    high, low = split(scaled)
+    sums = dot(select, high) + dot(select, low)
+    own_mean = jnp.sum(
+        jnp.where(lane == slot, jnp.broadcast_to(square, (slots, 128)), 0.0), axis=1, keepdims=True
+    ) * (1.0 / width)
+    own_weight = lax.rsqrt(own_mean + 1e-06)
+    own_high, own_low = split(pooled * own_weight)
+    sums_high, sums_low = split(sums)
+    square_high, square_low = split(sums * sums)
+    own = jnp.concatenate([own_high, own_low], axis=0)
+    cross = dot_nt(own, sums_high)
+    cross = cross[:slots] + cross[slots:] + dot_nt(own, sums_low)[:slots]
+    ones = jnp.ones((2 * slots, share), BF16)
+    norms = (dot_nt(ones, square_high) + dot_nt(ones, square_low))[:slots]
+    mixed = jnp.concatenate([cross, norms], axis=0)
+    final_part[...] = mixed
+    copies_fin = {}
+    for d in order:
+        copies_fin[d] = pltpu.make_async_remote_copy(
+            src_ref=final_part,
+            dst_ref=final_landed.at[d - 1],
+            send_sem=fin_send.at[d - 1],
+            recv_sem=fin_recv.at[d - 1],
+            device_id={"mp": (me + d) % mp},
+        )
+        copies_fin[d].start()
+    for d in reversed(order):
+        copies_fin[d].wait_recv()
+        mixed += final_landed[d - 1]
+    class_mean = mixed[slots : slots + 1] * (1.0 / width)
+    class_scale = lax.rsqrt(class_mean + 1e-06)
+    diagonal = lax.broadcasted_iota(jnp.int32, (classes, classes), 0) == lax.broadcasted_iota(
+        jnp.int32, (classes, classes), 1
+    )
+    column = jnp.sum(jnp.where(diagonal, class_scale, 0.0), axis=1, keepdims=True)
+    proto_ref[...] = sums * column
+    own_square = own_mean * own_weight * own_weight
+    distance = (own_square + class_mean * class_scale * class_scale) * width - 2.0 * (
+        mixed[:slots] * class_scale
+    )
+    episode = jnp.zeros((slots, 1), jnp.int32)
+    asked = jnp.zeros((slots, 1), jnp.int32)
+    for s in range(slots):
+        episode = jnp.where(row == s, episode_s[mine * slots + s], episode)
+        asked = jnp.where(row == s, flag_s[mine * slots + s], asked)
+    picked = jnp.zeros((slots, WAYS), F32)
+    for e in range(classes // WAYS):
+        picked = jnp.where(episode == e, distance[:, e * WAYS : (e + 1) * WAYS], picked)
+    logits = picked * (-1.0 / math.sqrt(width))
+    shifted = logits - jnp.max(logits, axis=1, keepdims=True)
+    result = shifted - jnp.log(jnp.sum(jnp.exp(shifted), axis=1, keepdims=True))
+    log_ref[...] = jnp.where(asked == 1, result, 0.0)
+
+    for d in order:
+        copies[d].wait_send()
+        copies_sq[d].wait_send()
+        copies_fin[d].wait_send()
+    for copy in sends + relays:
+        copy.wait_send()
+
+    def drain(d, carry):
+        share_square(d).wait_send()
+        return carry
+
+    lax.fori_loop(1, dp, drain, 0)
+
+
+def exchange(attended, token_sums, w_out, seq_lengths, episode_ids, class_ids, query_flags):
+    slots, share = token_sums.shape
+    mp, dp = lax.axis_size("mp"), lax.axis_size("dp")
+    total = episode_ids.shape[0]
+    classes = max(1, total // (2 * WAYS)) * WAYS
+    smem = pl.BlockSpec(memory_space=pltpu.SMEM)
+    vmem = pl.BlockSpec(memory_space=pltpu.VMEM)
+    dma = lambda n: pltpu.SemaphoreType.DMA((n,))
+    chips = dp // 2
+    return pl.pallas_call(
+        exchange_kernel,
+        out_shape=(
+            jax.ShapeDtypeStruct((slots, WAYS), F32),
+            jax.ShapeDtypeStruct((classes, share), F32),
+        ),
+        in_specs=[smem] * 3 + [vmem] * 6,
+        out_specs=(vmem, vmem),
+        scratch_shapes=[
+            pltpu.VMEM((mp, slots, share), F32),
+            pltpu.VMEM((mp - 1, slots, share), F32),
+            pltpu.VMEM((dp, slots, share), F32),
+            pltpu.VMEM((1, 128), F32),
+            pltpu.VMEM((mp - 1, 1, 128), F32),
+            pltpu.VMEM((dp, 1, 128), F32),
+            pltpu.VMEM((2 * slots, 128), F32),
+            pltpu.VMEM((mp - 1, 2 * slots, 128), F32),
+            dma(mp - 1),
+            dma(mp - 1),
+            dma(mp - 1),
+            dma(mp - 1),
+            dma(chips - 1),
+            dma(chips - 1),
+            dma(chips),
+            dma(chips),
+            dma(dp - 1),
+            dma(dp - 1),
+            dma(mp - 1),
+            dma(mp - 1),
+        ],
+        compiler_params=pltpu.CompilerParams(
+            collective_id=0, has_side_effects=True, vmem_limit_bytes=32 * 2**20
+        ),
+        name="exchange",
+    )(
+        seq_lengths,
+        episode_ids,
+        query_flags,
+        episode_ids,
+        class_ids,
+        query_flags,
+        attended,
+        token_sums,
+        w_out,
+    )
+
+
 def per_device(
     tokens,
     norm_gain,
@@ -252,58 +564,12 @@
     class_ids,
     query_flags,
 ):
-    width = tokens.shape[1]
-    slots = seq_starts.shape[0]
     attended, token_sums = local_part(
         tokens, norm_gain, w_query, w_key, w_value, seq_starts, seq_lengths
     )
-    high = attended.astype(BF16)
-    low = (attended - high.astype(F32)).astype(BF16)
-    both = dot(jnp.concatenate([high, low], axis=0), w_out)
-    head_part = both[:slots] + both[slots:]
-    mp = lax.axis_size("mp")
-    share = width // mp
-    pieces = head_part.reshape(slots, mp, share).transpose(1, 0, 2)
-    pieces = lax.all_to_all(pieces, "mp", split_axis=0, concat_axis=0, tiled=True)
-    pooled = (token_sums + pieces.sum(axis=0)) / seq_lengths.astype(F32)[:, None]
-    square = lax.psum(jnp.sum(pooled * pooled, axis=-1, keepdims=True), "mp")
-    embedded = pooled * lax.rsqrt(square / width + 1e-06)
-    everyone = lax.all_gather(embedded, "dp", axis=0, tiled=True)
-    seq_total = episode_ids.shape[0]
-    episodes = max(1, seq_total // (2 * WAYS))
-    classes = episodes * WAYS
-    global_class = episode_ids * WAYS + class_ids
-    class_range = jnp.arange(classes, dtype=jnp.int32)
-    select = (
-        (global_class[None, :] == class_range[:, None]) & (query_flags == 0)[None, :]
-    ).astype(F32)
-    highest = lax.Precision.HIGHEST
-    sums = jnp.dot(select, everyone, precision=highest)
-    cross = lax.dot_general(embedded, sums, (((1,), (1,)), ((), ())), precision=highest)
-    packed = jnp.concatenate([cross, jnp.sum(sums * sums, axis=1)[None, :]], axis=0)
-    packed = lax.psum(packed, "mp")
-    mean_square = packed[slots] / width
-    scale = lax.rsqrt(mean_square + 1e-06)
-    prototypes = sums * scale[:, None]
-    own_square = (square / width) / (square / width + 1e-06) * width
-    distance = (
-        own_square - 2.0 * packed[:slots] * scale[None, :] + (mean_square * scale * scale * width)[None, :]
-    )
-    own_first = lax.axis_index("dp") * slots
-    own_episode = lax.dynamic_slice_in_dim(episode_ids, own_first, slots, 0)
-    own_query = lax.dynamic_slice_in_dim(query_flags, own_first, slots, 0)
-    picked = jnp.sum(
-        jnp.where(
-            own_episode[:, None, None] == jnp.arange(episodes, dtype=jnp.int32)[None, :, None],
-            distance.reshape(slots, episodes, WAYS),
-            0.0,
-        ),
-        axis=1,
-    )
-    logits = -picked / math.sqrt(width)
-    shifted = logits - jnp.max(logits, axis=-1, keepdims=True)
-    log_probs = shifted - jnp.log(jnp.sum(jnp.exp(shifted), axis=-1, keepdims=True))
-    return jnp.where(own_query[:, None] == 1, log_probs, 0.0), prototypes
+    return exchange(
+        attended, token_sums, w_out, seq_lengths, episode_ids, class_ids, query_flags
+    )
 
 
 def solution(mesh):

time: 127 us -> 62.8 us (0.49)
  waiting for transfers between devices: 50.2 us -> 0 us
  Pallas kernels: 23.6 us -> 52 us
  blocking collectives: 15.7 us -> 0 us
  between operations: 14.1 us -> 0.7 us
  starting transfers between devices: 5.86 us -> 0 us
  other arithmetic: 3.81 us -> 0 us
  matrix products: 3.74 us -> 0 us
    all_gather x1 -> x0, waiting for transfers between devices: 45.4 us -> none  [per_device(): everyone = lax.all_gather(embedded, 'dp', axis=0, tiled=True)]
    pallas_call x0 -> x1, Pallas kernels: none -> 28.4 us  [exchange(): pl.pallas_call(exchange_kernel, out_shape=(jax.ShapeDtypeStruct((slots, W...]
    psum x2 -> x0, blocking collectives: 15.7 us -> none  [the longest x1 8.78 us: per_device(): packed = lax.psum(packed, 'mp')]
    all_to_all x1 -> x0, starting transfers between devices: 5.86 us -> none  [per_device(): lax.all_to_all(pieces, 'mp', split_axis=0, concat_axis=0, tiled=True)]
    all_to_all x1 -> x0, waiting for transfers between devices: 4.82 us -> none  [per_device(): lax.all_to_all(pieces, 'mp', split_axis=0, concat_axis=0, tiled=True)]
    dot_general x3 -> x0, matrix products: 3.74 us -> none  [the longest x1 1.82 us: per_device(): sums = jnp.dot(select, everyone, precision=highest)]
    mul x2 -> x0, other arithmetic: 1.59 us -> none  [the longest x1 0.9 us: per_device(): prototypes = sums * scale[:, None]]
    unnamed x24, local copies, waits for them, and re-layouts: 7.62 us -> 8.98 us
  transfers between devices with their start and end apart: 2 -> 0, of which waited for: 2 -> 0; matrix products, arithmetic and copies ran while one was open for 0% -> 0% of each run, Pallas kernels for 0% -> 0%
where the time goes in v2:
time: 62.8 us; the launch traced here: 62.4 us
  Pallas kernels  52 us (83%)
  local copies, waits for them, and re-layouts  9.69 us (15%)
  between operations  0.7 us (1%)
    pallas_call x1, Pallas kernels, exchange(): pl.pallas_call(exchange_kernel, out_shape=(jax.ShapeDtypeStruct((slots, W...  28.4 us
    pallas_call x1, Pallas kernels, local_part(): pl.pallas_call(local_kernel, grid=(STEPS,), out_shape=(jax.ShapeDtypeStru...  23.6 us
    unnamed x24, local copies, waits for them, and re-layouts  8.98 us

profile of v2, /device:TPU:1, one launch (start us, length us, event | category | flops | bytes accessed | tf_op | source)
XLA Modules:
  0.0 62.4 jit_solution(5173824194026205399)
XLA Ops:
  0.6 0.7 %reshape.7.gain = bf16[1,4096]{1,0:T(2,128)(2,1)S(1)} reshape(bf16[4096]{0:T(1024)(128)(2,1)} %param.14) | data formatting | bytes 16384 | tf_op jit(solution)/shard_map/reshape | solution.py:232
  1.3 0.0 copy-start
  1.4 2.2 %copy-done = bf16[4096,512]{1,0:T(8,128)(2,1)S(1)} copy-done((bf16[4096,512]{1,0:T(8,128)(2,1)S(1)}, bf16[4096,512]{1,0:T(8,128)(2,1)}, u32[]{:S(2)}) %copy-start) | copy-done | bytes 4194328
  3.5 0.0 copy-start.2
  3.5 1.2 %copy-done.2 = bf16[4096,128]{1,0:T(8,128)(2,1)S(1)} copy-done((bf16[4096,128]{1,0:T(8,128)(2,1)S(1)}, bf16[4096,128]{1,0:T(8,128)(2,1)}, u32[]{:S(2)}) %copy-start.2) | copy-done | bytes 1048600
  4.8 0.0 copy-start.3
  4.8 1.2 %copy-done.3 = bf16[4096,128]{1,0:T(8,128)(2,1)S(1)} copy-done((bf16[4096,128]{1,0:T(8,128)(2,1)S(1)}, bf16[4096,128]{1,0:T(8,128)(2,1)}, u32[]{:S(2)}) %copy-start.3) | copy-done | bytes 1048600
  6.0 0.0 copy-start.4
  6.0 0.8 %copy-done.4 = f32[2,64,128]{2,1,0:T(8,128)S(1)} copy-done((f32[2,64,128]{2,1,0:T(8,128)S(1)}, f32[2,64,128]{2,1,0:T(8,128)}, u32[]{:S(2)}) %copy-start.4) | copy-done | bytes 65560
  6.8 0.0 copy-start.5
  6.8 0.8 %copy-done.5 = f32[4,24,128]{2,1,0:T(8,128)S(1)} copy-done((f32[4,24,128]{2,1,0:T(8,128)S(1)}, f32[4,24,128]{2,1,0:T(8,128)}, u32[]{:S(2)}) %copy-start.5) | copy-done | bytes 49176
  7.6 0.0 copy-start.8
  7.6 0.7 %copy-done.8 = s32[8]{0:T(128)S(1)} copy-done((s32[8]{0:T(128)S(1)}, s32[8]{0:T(128)}, u32[]{:S(2)}) %copy-start.8) | copy-done | bytes 56
  8.3 0.0 copy-start.10
  8.3 0.7 %copy-done.10 = s32[8]{0:T(128)S(1)} copy-done((s32[8]{0:T(128)S(1)}, s32[8]{0:T(128)}, u32[]{:S(2)}) %copy-start.10) | copy-done | bytes 56
  8.9 0.0 copy-start.1
  8.9 23.6 %local_part.1 = (f32[8,512]{1,0:T(8,128)S(1)}, f32[8,1024]{1,0:T(8,128)S(1)}) custom-call(s32[8]{0:T(128)S(1)} %copy-done.10, s32[8]{0:T(128)S(1)} %copy-done.8, bf16[1,4096]{1,0:T(2,128)(2,1)S(1)} %reshape.7.gain, f32[2,64,128]{2,1,0:T(8,128)S(1)} %copy-done.4, f32[4,24,128]{2,1,0:T(8,128)S(1)} %copy-done.5, bf16[1536,4096]{1,0:T(8,128)(2,1)} %x_ref.1, ...), custom_call_target="tpu_custom_call" | custom-call | tf_op jit(solution)/shard_map/local_part/pallas_call | solution.py:197
  32.5 0.0 copy-done.1
  32.5 0.0 copy-done.6
  32.6 0.0 copy-done.7
  32.6 0.0 copy-done.9
  32.6 28.4 %exchange.1 = (f32[8,32]{1,0:T(8,128)S(1)}, f32[128,1024]{1,0:T(8,128)S(1)}) custom-call(s32[8]{0:T(128)S(1)} %copy-done.8, s32[256]{0:T(256)S(1)} %copy-done.6, s32[256]{0:T(256)S(1)} %copy-done.7, s32[256]{0:T(256)S(1)} %copy-done.6, s32[256]{0:T(256)S(1)} %copy-done.9, s32[256]{0:T(256)S(1)} %copy-done.7, f32[8,512]{1,0:T(8,128)S(1)} %get-tuple-element.4.att_ref, ...), custom_call_target="tpu_custom_call" | custom-call | tf_op jit(solution)/shard_map/exchange/pallas_call | solution.py:507
  61.0 0.6 copy.17
  61.6 0.8 %copy.18 = f32[128,1024]{1,0:T(8,128)} copy(f32[128,1024]{1,0:T(8,128)S(1)} %get-tuple-element.9) | data formatting | bytes 1048576
  (3 shorter events, 0.0 us)
Async XLA Ops:
  1.3 2.2 %copy-start = (bf16[4096,512]{1,0:T(8,128)(2,1)S(1)}, bf16[4096,512]{1,0:T(8,128)(2,1)}, u32[]{:S(2)}) copy-start(bf16[4096,512]{1,0:T(8,128)(2,1)} %wq_ref.1) | copy-start | bytes 12582916
  3.5 1.2 %copy-start.2 = (bf16[4096,128]{1,0:T(8,128)(2,1)S(1)}, bf16[4096,128]{1,0:T(8,128)(2,1)}, u32[]{:S(2)}) copy-start(bf16[4096,128]{1,0:T(8,128)(2,1)} %wk_ref.1) | copy-start | bytes 3145732
  4.8 1.2 %copy-start.3 = (bf16[4096,128]{1,0:T(8,128)(2,1)S(1)}, bf16[4096,128]{1,0:T(8,128)(2,1)}, u32[]{:S(2)}) copy-start(bf16[4096,128]{1,0:T(8,128)(2,1)} %wv_ref.1) | copy-start | bytes 3145732
  6.0 0.8 %copy-start.4 = (f32[2,64,128]{2,1,0:T(8,128)S(1)}, f32[2,64,128]{2,1,0:T(8,128)}, u32[]{:S(2)}) copy-start(f32[2,64,128]{2,1,0:T(8,128)} %constant.4.clone.fine) | copy-start | bytes 196612
  6.8 0.8 %copy-start.5 = (f32[4,24,128]{2,1,0:T(8,128)S(1)}, f32[4,24,128]{2,1,0:T(8,128)}, u32[]{:S(2)}) copy-start(f32[4,24,128]{2,1,0:T(8,128)} %constant.5.clone.coarse) | copy-start | bytes 147460
  7.6 0.7 %copy-start.8 = (s32[8]{0:T(128)S(1)}, s32[8]{0:T(128)}, u32[]{:S(2)}) copy-start(s32[8]{0:T(128)} %lengths.3) | copy-start | bytes 100
  8.3 0.7 %copy-start.10 = (s32[8]{0:T(128)S(1)}, s32[8]{0:T(128)}, u32[]{:S(2)}) copy-start(s32[8]{0:T(128)} %starts.1) | copy-start | bytes 100
  8.9 23.6 %copy-start.1 = (bf16[512,4096]{1,0:T(8,128)(2,1)S(1)}, bf16[512,4096]{1,0:T(8,128)(2,1)}, u32[]{:S(2)}) copy-start(bf16[512,4096]{1,0:T(8,128)(2,1)} %wo_ref.1) | copy-start | bytes 12582916
  8.9 23.6 %copy-start.6 = (s32[256]{0:T(256)S(1)}, s32[256]{0:T(256)}, u32[]{:S(2)}) copy-start(s32[256]{0:T(256)} %episode_v.1) | copy-start | bytes 3076
  8.9 23.6 %copy-start.7 = (s32[256]{0:T(256)S(1)}, s32[256]{0:T(256)}, u32[]{:S(2)}) copy-start(s32[256]{0:T(256)} %flag_v.1) | copy-start | bytes 3076
  8.9 23.6 %copy-start.9 = (s32[256]{0:T(256)S(1)}, s32[256]{0:T(256)}, u32[]{:S(2)}) copy-start(s32[256]{0:T(256)} %class_v.1) | copy-start | bytes 3076

commit v3 on v0

v3 whole, which is shorter than its diff:
```python
import functools
import math

import jax
import jax.numpy as jnp
import numpy as np
from jax import lax
from jax.experimental import pallas as pl
from jax.experimental.pallas import tpu as pltpu
from jax.sharding import PartitionSpec as P

HEAD_DIM = 128
WAYS = 32
ROPE_BASE = 500000.0
LONGEST = 640
STEPS = 8
AHEAD = 3
TILE = 128
ONES = 16
EARLY = 4
SHORTEST = 128
FAR = -(2.0**100)
F32 = jnp.float32
BF16 = jnp.bfloat16


def rope_tables(rows, block):
    half = HEAD_DIM // 2
    frequency = ROPE_BASE ** (-(np.arange(half, dtype=np.float64) * 2.0 / HEAD_DIM))
    frequency = np.concatenate([frequency, frequency])[None, :]
    sign = np.where(np.arange(HEAD_DIM) < half, -1.0, 1.0)[None, :]
    fine = np.arange(block, dtype=np.float64)[:, None] * frequency
    coarse = np.arange(0, rows, block, dtype=np.float64)[:, None] * frequency
    fine_table = np.stack([np.cos(fine), np.sin(fine)])
    coarse_table = np.stack(
        [np.cos(coarse), np.sin(coarse), sign * np.cos(coarse), sign * np.sin(coarse)]
    )
    return fine_table.astype(np.float32), coarse_table.astype(np.float32)


def dot(a, b):
    return jnp.dot(a, b, preferred_element_type=F32)


def dot_nt(a, b):
    return lax.dot_general(a, b, (((1,), (1,)), ((), ())), preferred_element_type=F32)


def split(a):
    high = a.astype(BF16)
    return high, (a - high.astype(F32)).astype(BF16)


def fold(a):
    half = a.shape[1] // 2
    return jnp.concatenate([a[:, :half], a[:, half:]], axis=0)


def whole_kernel(
    starts_h,
    lengths_h,
    episode_h,
    class_h,
    flag_h,
    gain_h,
    fine_h,
    coarse_h,
    x_h,
    wq_h,
    wk_h,
    wv_h,
    wo_h,
    log_ref,
    proto_ref,
    starts,
    lengths,
    episode_s,
    flag_s,
    episode_v,
    class_v,
    flag_v,
    gain,
    fine,
    coarse,
    x_v,
    w_v,
    wo_v,
    acc,
    squares,
    member,
    qs,
    ks,
    vt,
    ot,
    part,
    landed,
    everyone,
    square_part,
    square_landed,
    row_squares,
    final_part,
    final_landed,
    small_sem,
    x_sem,
    wq_sem,
    wk_sem,
    wv_sem,
    late_sem,
    wo_sem,
    rs_send,
    rs_recv,
    sq_send,
    sq_recv,
    ag_send,
    ag_recv,
    relay_send,
    relay_recv,
    all_send,
    all_recv,
    fin_send,
    fin_recv,
):
    mp = lax.axis_size("mp")
    dp = lax.axis_size("dp")
    me = lax.axis_index("mp")
    mine = lax.axis_index("dp")
    rows, width = x_v.shape
    slots = starts.shape[0]
    heads = wq_h.shape[1] // HEAD_DIM
    depth = width // STEPS
    tiles = rows // TILE
    share = width // mp
    late = slots - EARLY
    cut = rows - late * SHORTEST
    late_from = EARLY * SHORTEST
    block = 512

    smalls = [
        pltpu.make_async_copy(source, target, small_sem.at[i])
        for i, (source, target) in enumerate(
            [
                (gain_h, gain),
                (starts_h, starts),
                (lengths_h, lengths),
                (fine_h, fine),
                (coarse_h, coarse),
                (episode_h, episode_s),
                (flag_h, flag_s),
                (episode_h, episode_v),
                (class_h, class_v),
                (flag_h, flag_v),
            ]
        )
    ]

    def chunk_copies(c):
        at = pl.ds(c * depth, depth)
        q, k = heads * HEAD_DIM, HEAD_DIM
        return [
            pltpu.make_async_copy(
                x_h.at[pl.ds(0, cut), at], x_v.at[pl.ds(0, cut), at], x_sem.at[c]
            ),
            pltpu.make_async_copy(wq_h.at[at, :], w_v.at[at, pl.ds(0, q)], wq_sem.at[c]),
            pltpu.make_async_copy(wk_h.at[at, :], w_v.at[at, pl.ds(q, k)], wk_sem.at[c]),
            pltpu.make_async_copy(wv_h.at[at, :], w_v.at[at, pl.ds(q + k, k)], wv_sem.at[c]),
        ]

    smalls[0].start()
    for copy in chunk_copies(0):
        copy.start()
    for copy in smalls[1:]:
        copy.start()
    for c in range(1, AHEAD):
        for copy in chunk_copies(c):
            copy.start()
    late_copy = pltpu.make_async_copy(
        x_h.at[pl.ds(cut, rows - cut), :], x_v.at[pl.ds(cut, rows - cut), :], late_sem.at[0]
    )
    wo_copy = pltpu.make_async_copy(wo_h, wo_v, wo_sem.at[0])

    barrier = pltpu.get_barrier_semaphore()
    for d in range(1, mp):
        pl.semaphore_signal(barrier, inc=1, device_id={"mp": (me + d) % mp})

    def greet(d, carry):
        pl.semaphore_signal(barrier, inc=1, device_id={"dp": (mine + d) % dp})
        return carry

    lax.fori_loop(1, dp, greet, 0)

    def project(first, c, fresh):
        at = pl.ds(first, block)
        deep = pl.ds(c * depth, depth)
        x = x_v[at, deep]
        wide = x.astype(F32)
        wide = wide * wide
        total = wide[:, 0:128]
        for i in range(1, depth // 128):
            total += wide[:, i * 128 : (i + 1) * 128]
        value = dot(x * gain[deep].reshape(1, depth), w_v[deep, :])
        if fresh:
            squares[at, :] = total
            acc[at, :] = value
        else:
            squares[at, :] += total
            acc[at, :] += value

    scale = math.log2(math.e) / math.sqrt(HEAD_DIM)

    def row_scale_of(at):
        return lax.rsqrt(jnp.sum(squares[at, :], axis=1, keepdims=True) * (1.0 / width) + 1e-05)

    def slot_bounds(shape, axis):
        index = lax.broadcasted_iota(jnp.int32, shape, axis)
        first = jnp.full(shape, rows, jnp.int32)
        last = jnp.zeros(shape, jnp.int32)
        for s in range(slots):
            first = jnp.where(index == s, starts[s], first)
            last = jnp.where(index == s, starts[s] + lengths[s], last)
        return first, last

    def prepare(i):
        first, last = slot_bounds((1, 128), 1)
        fine_cos, fine_sin = fine[0], fine[1]
        for h in range(TILE // 64):
            low = i * TILE + h * 64
            at = pl.ds(low, 64)
            row_scale = row_scale_of(at)
            b = low // 64
            cos_a, sin_a = coarse[0, b : b + 1, :], coarse[1, b : b + 1, :]
            cos_s, sin_s = coarse[2, b : b + 1, :], coarse[3, b : b + 1, :]
            cosine = (cos_a * fine_cos - sin_a * fine_sin) * row_scale
            sine = (sin_s * fine_cos + cos_s * fine_sin) * row_scale
            token = low + lax.broadcasted_iota(jnp.int32, (64, 128), 0)
            inside = (token >= first) & (token < last)
            q_mark = jnp.where(inside, 1.0, 0.0).astype(BF16)
            k_mark = jnp.where(inside, 0.0, FAR).astype(BF16)
            for n in range(heads):
                v = acc[at, n * 128 : (n + 1) * 128]
                v = v * cosine + pltpu.roll(v, 64, 1) * sine
                to = pl.ds(n * TILE + h * 64, 64)
                qs[i, to, 0:128] = v.astype(BF16)
                qs[i, to, 128:256] = q_mark
            v = acc[at, heads * 128 : (heads + 1) * 128] * scale
            v = v * cosine + pltpu.roll(v, 64, 1) * sine
            ks[at, 0:128] = v.astype(BF16)
            ks[at, 128:256] = k_mark
        at = pl.ds(i * TILE, TILE)
        v = acc[at, (heads + 1) * 128 : (heads + 2) * 128] * row_scale_of(at)
        vt[0:128, at] = v.T.astype(BF16)
        vt[128 : 128 + ONES, at] = jnp.ones((ONES, TILE), BF16)

    def attend(i):
        key = lax.broadcasted_iota(jnp.int32, (TILE, heads * TILE), 0)
        query = lax.broadcasted_iota(jnp.int32, (TILE, heads * TILE), 1) % TILE
        begin = max(0, i * TILE - LONGEST)
        before = i * TILE - begin
        s = dot_nt(ks[begin : (i + 1) * TILE, :], qs[i])
        own = jnp.where(key <= query, s[before:], FAR)
        peak = jnp.max(own, axis=0, keepdims=True)
        if before:
            peak = jnp.maximum(peak, jnp.max(s[:before], axis=0, keepdims=True))
        e = jnp.exp2(own - peak).astype(BF16)
        if before:
            e = jnp.concatenate([jnp.exp2(s[:before] - peak).astype(BF16), e], axis=0)
        o = dot(vt[:, begin : (i + 1) * TILE], e)
        o = (o[0:128] / o[128:129]).astype(BF16)
        for n in range(heads):
            ot[n * 128 : (n + 1) * 128, i * TILE : (i + 1) * TILE] = o[:, n * TILE : (n + 1) * TILE]

    def head_part(group):
        span = slice(0, cut) if group == 0 else slice(late_from, rows)
        pick = slice(0, EARLY) if group == 0 else slice(EARLY, slots)
        high, low = split(dot_nt(member[:, span], ot[:, span])[pick])
        stacked = jnp.concatenate([high, low], axis=0)
        for r in range(mp):
            both = dot(stacked, wo_v[:, r * share : (r + 1) * share])
            n = both.shape[0] // 2
            part[group, r] = fold(both[:n] + both[n:])

    def token_part(group):
        span = slice(0, cut) if group == 0 else slice(late_from, rows)
        pick = slice(0, EARLY) if group == 0 else slice(EARLY, slots)
        own = pl.ds(pl.multiple_of(me * share, share), share)
        return fold(dot(member[:, span], x_v[span, own])[pick])

    order = sorted(range(1, mp), key=lambda d: -min(d, mp - d))

    def reduce_copies(group):
        return {
            d: pltpu.make_async_remote_copy(
                src_ref=part.at[group, (me + d) % mp],
                dst_ref=landed.at[group, d - 1],
                send_sem=rs_send.at[group, d - 1],
                recv_sem=rs_recv.at[group, d - 1],
                device_id={"mp": (me + d) % mp},
            )
            for d in order
        }

    def reduced(group, copies, tokens_sum):
        value = tokens_sum + part[group, me]
        for d in reversed(order):
            copies[d].wait_recv()
            value += landed[group, d - 1]
        size = value.shape[0]
        row = lax.broadcasted_iota(jnp.int32, (size, 1), 0)
        count = jnp.ones((size, 1), jnp.int32)
        for s in range(size):
            count = jnp.where(row == s, lengths[group * EARLY + s % (size // 2)], count)
        return value / count.astype(F32)

    side = int(math.isqrt(dp // 2))
    x, y, core = mine // (2 * side), (mine // 2) % side, mine % 2
    partner = mine + 1 - 2 * core

    def at_offset(dx, dy):
        return (((x + dx + side) % side) * side + (y + dy + side) % side) * 2 + core

    reach = lambda o: min(o[0], side - o[0]) + min(o[1], side - o[1])
    offsets = [(dx, dy) for dx in range(side) for dy in range(side) if dx or dy]
    offsets = sorted(offsets, key=lambda o: -reach(o))

    def gather_copy(group, i):
        return pltpu.make_async_remote_copy(
            src_ref=everyone.at[group, mine],
            dst_ref=everyone.at[group, mine],
            send_sem=ag_send.at[group, i],
            recv_sem=ag_recv.at[group, i],
            device_id={"dp": at_offset(*offsets[i])},
        )

    def relay_copy(group, i):
        source = mine if i == len(offsets) else at_offset(-offsets[i][0], -offsets[i][1])
        return pltpu.make_async_remote_copy(
            src_ref=everyone.at[group, source],
            dst_ref=everyone.at[group, source],
            send_sem=relay_send.at[group, i],
            recv_sem=relay_recv.at[group, i],
            device_id={"dp": partner},
        )

    def gather(group):
        for i in range(len(offsets)):
            gather_copy(group, i).start()
        relay_copy(group, len(offsets)).start()

    def relay(group):
        for i in reversed(range(len(offsets))):
            gather_copy(group, i).wait_recv()
            relay_copy(group, i).start()

    for c in range(STEPS):
        if c == 0:
            smalls[0].wait()
        for copy in chunk_copies(c):
            copy.wait()
        if c + AHEAD < STEPS:
            for copy in chunk_copies(c + AHEAD):
                copy.start()
        if c + AHEAD == STEPS:
            late_copy.start()
        if c + AHEAD == STEPS + 1:
            wo_copy.start()
        for first in range(0, cut, block):
            project(first, c, c == 0)
    for copy in smalls[1:]:
        copy.wait()
    token = lax.broadcasted_iota(jnp.int32, (ONES, rows), 1)
    first, last = slot_bounds((ONES, rows), 0)
    member[...] = jnp.where((token >= first) & (token < last), 1.0, 0.0).astype(BF16)
    for i in range(cut // TILE):
        prepare(i)
    for i in range(cut // TILE):
        attend(i)
    wo_copy.wait()
    head_part(0)
    pl.semaphore_wait(barrier, mp - 1 + dp - 1)
    reduce_early = reduce_copies(0)
    for d in order:
        reduce_early[d].start()

    late_copy.wait()
    for c in range(STEPS):
        for first in range(cut, rows, block):
            project(first, c, c == 0)
    tokens_early = token_part(0)
    pooled_early = reduced(0, reduce_early, tokens_early)
    everyone[0, mine] = pooled_early
    gather(0)

    for i in range(cut // TILE, tiles):
        prepare(i)
    for i in range(cut // TILE, tiles):
        attend(i)
    head_part(1)
    reduce_late = reduce_copies(1)
    for d in order:
        reduce_late[d].start()
    tokens_late = token_part(1)
    relay(0)
    pooled_late = reduced(1, reduce_late, tokens_late)
    everyone[1, mine] = pooled_late
    gather(1)

    lane = lax.broadcasted_iota(jnp.int32, (slots, 128), 1)
    slot = lax.broadcasted_iota(jnp.int32, (slots, 128), 0)
    parts = []
    for group, value in enumerate((pooled_early, pooled_late)):
        total = jnp.sum(value * value, axis=1, keepdims=True)
        parts.append(jnp.where(lane % EARLY == slot % EARLY, total, 0.0))
    parts = jnp.where(lane < EARLY, parts[0], jnp.where(lane < slots, parts[1], 0.0))
    square = jnp.sum(parts, axis=0, keepdims=True)
    square_part[...] = square
    copies_sq = {}
    for d in order:
        copies_sq[d] = pltpu.make_async_remote_copy(
            src_ref=square_part,
            dst_ref=square_landed.at[d - 1],
            send_sem=sq_send.at[d - 1],
            recv_sem=sq_recv.at[d - 1],
            device_id={"mp": (me + d) % mp},
        )
        copies_sq[d].start()
    for d in reversed(order):
        copies_sq[d].wait_recv()
        square += square_landed[d - 1]
    row_squares[mine] = square

    def share_square(d):
        return pltpu.make_async_remote_copy(
            src_ref=row_squares.at[mine],
            dst_ref=row_squares.at[mine],
            send_sem=all_send.at[d - 1],
            recv_sem=all_recv.at[d - 1],
            device_id={"dp": (mine + d) % dp},
        )

    def start_square(d, carry):
        share_square(d).start()
        return carry

    lax.fori_loop(1, dp, start_square, 0)
    relay(1)

    total = dp * slots
    classes = proto_ref.shape[0]
    named = episode_v[...] * WAYS + class_v[...]
    named = jnp.where(flag_v[...] == 0, named, -1).reshape(1, total)
    kind = lax.broadcasted_iota(jnp.int32, (classes, total), 0)
    select = jnp.where(kind == named, 1.0, 0.0).astype(BF16)

    def wait_square(d, carry):
        share_square(d).wait_recv()
        return carry

    lax.fori_loop(1, dp, wait_square, 0)
    spread = jnp.where(
        lax.broadcasted_iota(jnp.int32, (dp, slots, 128), 2)
        == lax.broadcasted_iota(jnp.int32, (dp, slots, 128), 1),
        row_squares[...],
        0.0,
    )
    weight = lax.rsqrt(jnp.sum(spread, axis=2, keepdims=True) * (1.0 / width) + 1e-06)
    for group in range(2):
        for i in range(len(offsets) + 1):
            relay_copy(group, i).wait_recv()

    def unfold(early, late):
        axis = early.ndim - 2
        a = [lax.slice_in_dim(early, h * EARLY, (h + 1) * EARLY, axis=axis) for h in range(2)]
        b = [lax.slice_in_dim(late, h * EARLY, (h + 1) * EARLY, axis=axis) for h in range(2)]
        return jnp.concatenate(
            [jnp.concatenate([a[h], b[h]], axis=axis) for h in range(2)], axis=axis + 1
        )

    scaled = (unfold(everyone[0], everyone[1]) * weight).reshape(total, share)
    high, low = split(scaled)
    sums = dot(select, high) + dot(select, low)
    own_mean = jnp.sum(
        jnp.where(lane == slot, jnp.broadcast_to(square, (slots, 128)), 0.0), axis=1, keepdims=True
    ) * (1.0 / width)
    own_weight = lax.rsqrt(own_mean + 1e-06)
    own_high, own_low = split(unfold(pooled_early, pooled_late) * own_weight)
    sums_high, sums_low = split(sums)
    square_high, square_low = split(sums * sums)
    own = jnp.concatenate([own_high, own_low], axis=0)
    cross = dot_nt(own, sums_high)
    cross = cross[:slots] + cross[slots:] + dot_nt(own, sums_low)[:slots]
    ones = jnp.ones((2 * slots, share), BF16)
    norms = (dot_nt(ones, square_high) + dot_nt(ones, square_low))[:slots]
    mixed = jnp.concatenate([cross, norms], axis=0)
    final_part[...] = mixed
    copies_fin = {}
    for d in order:
        copies_fin[d] = pltpu.make_async_remote_copy(
            src_ref=final_part,
            dst_ref=final_landed.at[d - 1],
            send_sem=fin_send.at[d - 1],
            recv_sem=fin_recv.at[d - 1],
            device_id={"mp": (me + d) % mp},
        )
        copies_fin[d].start()
    for d in reversed(order):
        copies_fin[d].wait_recv()
        mixed += final_landed[d - 1]
    class_mean = mixed[slots : slots + 1] * (1.0 / width)
    class_scale = lax.rsqrt(class_mean + 1e-06)
    diagonal = lax.broadcasted_iota(jnp.int32, (classes, classes), 0) == lax.broadcasted_iota(
        jnp.int32, (classes, classes), 1
    )
    column = jnp.sum(jnp.where(diagonal, class_scale, 0.0), axis=1, keepdims=True)
    proto_ref[...] = sums * column
    own_square = own_mean * own_weight * own_weight
    distance = (own_square + class_mean * class_scale * class_scale) * width - 2.0 * (
        mixed[:slots] * class_scale
    )
    row = lax.broadcasted_iota(jnp.int32, (slots, 1), 0)
    episode = jnp.zeros((slots, 1), jnp.int32)
    asked = jnp.zeros((slots, 1), jnp.int32)
    for s in range(slots):
        episode = jnp.where(row == s, episode_s[mine * slots + s], episode)
        asked = jnp.where(row == s, flag_s[mine * slots + s], asked)
    picked = jnp.zeros((slots, WAYS), F32)
    for e in range(classes // WAYS):
        picked = jnp.where(episode == e, distance[:, e * WAYS : (e + 1) * WAYS], picked)
    logits = picked * (-1.0 / math.sqrt(width))
    shifted = logits - jnp.max(logits, axis=1, keepdims=True)
    result = shifted - jnp.log(jnp.sum(jnp.exp(shifted), axis=1, keepdims=True))
    log_ref[...] = jnp.where(asked == 1, result, 0.0)

    for d in order:
        reduce_early[d].wait_send()
        reduce_late[d].wait_send()
        copies_sq[d].wait_send()
        copies_fin[d].wait_send()
    for group in range(2):
        for i in range(len(offsets)):
            gather_copy(group, i).wait_send()
        for i in range(len(offsets) + 1):
            relay_copy(group, i).wait_send()

    def drain(d, carry):
        share_square(d).wait_send()
        return carry

    lax.fori_loop(1, dp, drain, 0)


def per_device(
    tokens,
    norm_gain,
    w_query,
    w_key,
    w_value,
    w_out,
    seq_starts,
    seq_lengths,
    episode_ids,
    class_ids,
    query_flags,
):
    rows, width = tokens.shape
    slots = seq_starts.shape[0]
    inner = w_query.shape[1]
    heads = inner // HEAD_DIM
    columns = inner + w_key.shape[1] + w_value.shape[1]
    mp, dp = lax.axis_size("mp"), lax.axis_size("dp")
    share = width // mp
    tiles = rows // TILE
    total = episode_ids.shape[0]
    classes = max(1, total // (2 * WAYS)) * WAYS
    chips = dp // 2
    fine, coarse = rope_tables(rows, 64)
    hbm = pl.BlockSpec(memory_space=pltpu.HBM)
    vmem = pl.BlockSpec(memory_space=pltpu.VMEM)
    dma = lambda *n: pltpu.SemaphoreType.DMA(n)
    ints = lambda n: pltpu.SMEM((n,), jnp.int32)
    return pl.pallas_call(
        whole_kernel,
        out_shape=(
            jax.ShapeDtypeStruct((slots, WAYS), F32),
            jax.ShapeDtypeStruct((classes, share), F32),
        ),
        in_specs=[hbm] * 13,
        out_specs=(vmem, vmem),
        scratch_shapes=[
            ints(slots),
            ints(slots),
            ints(total),
            ints(total),
            pltpu.VMEM((total,), jnp.int32),
            pltpu.VMEM((total,), jnp.int32),
            pltpu.VMEM((total,), jnp.int32),
            pltpu.VMEM((width,), BF16),
            pltpu.VMEM(fine.shape, F32),
            pltpu.VMEM(coarse.shape, F32),
            pltpu.VMEM((rows, width), BF16),
            pltpu.VMEM((width, columns), BF16),
            pltpu.VMEM((inner, width), BF16),
            pltpu.VMEM((rows, columns), F32),
            pltpu.VMEM((rows, 128), F32),
            pltpu.VMEM((ONES, rows), BF16),
            pltpu.VMEM((tiles, heads * TILE, 256), BF16),
            pltpu.VMEM((rows, 256), BF16),
            pltpu.VMEM((128 + ONES, rows), BF16),
            pltpu.VMEM((inner, rows), BF16),
            pltpu.VMEM((2, mp, slots, share // 2), F32),
            pltpu.VMEM((2, mp - 1, slots, share // 2), F32),
            pltpu.VMEM((2, dp, slots, share // 2), F32),
            pltpu.VMEM((1, 128), F32),
            pltpu.VMEM((mp - 1, 1, 128), F32),
            pltpu.VMEM((dp, 1, 128), F32),
            pltpu.VMEM((2 * slots, 128), F32),
            pltpu.VMEM((mp - 1, 2 * slots, 128), F32),
            dma(10),
            dma(STEPS),
            dma(STEPS),
            dma(STEPS),
            dma(STEPS),
            dma(1),
            dma(1),
            dma(2, mp - 1),
            dma(2, mp - 1),
            dma(mp - 1),
            dma(mp - 1),
            dma(2, chips - 1),
            dma(2, chips - 1),
            dma(2, chips),
            dma(2, chips),
            dma(dp - 1),
            dma(dp - 1),
            dma(mp - 1),
            dma(mp - 1),
        ],
        compiler_params=pltpu.CompilerParams(
            collective_id=0, has_side_effects=True, vmem_limit_bytes=60 * 2**20
        ),
        name="whole",
    )(
        seq_starts,
        seq_lengths,
        episode_ids,
        class_ids,
        query_flags,
        norm_gain,
        jnp.asarray(fine),
        jnp.asarray(coarse),
        tokens,
        w_query,
        w_key,
        w_value,
        w_out,
    )


def solution(mesh):
    placed = (
        P("dp", None),
        P(),
        P(None, "mp"),
        P(None, "mp"),
        P(None, "mp"),
        P("mp", None),
        P("dp"),
        P("dp"),
        P(),
        P(),
        P(),
    )
    return jax.shard_map(
        per_device,
        mesh=mesh,
        in_specs=placed,
        out_specs=(P("dp", None), P(None, "mp")),
        check_vma=False,
    )
```

time: 174 us -> 53.6 us (0.31); the launches traced: 171 us -> 53.2 us
  Pallas kernels: 0 us -> 49.4 us
  waiting for transfers between devices: 46.9 us -> 0 us
  matrix products: 45.4 us -> 0 us
  other arithmetic: 39.2 us -> 0 us
  blocking collectives: 14.5 us -> 0 us
  between operations: 14.7 us -> 0.64 us
  local copies, waits for them, and re-layouts: 10.1 us -> 3.15 us
    pallas_call x0 -> x1, Pallas kernels: none -> 49.4 us  [per_device(): pl.pallas_call(whole_kernel, out_shape=(jax.ShapeDtypeStruct((slots, WAYS...]
    all_gather x1 -> x0, waiting for transfers between devices: 46.9 us -> none  [per_device(): lax.all_gather(embedded, 'dp', axis=0, tiled=True)]
    dot_general x14 -> x0, matrix products: 45.4 us -> none  [the longest x1 9.66 us: per_device(): jnp.dot(normed, w_query, preferred_element_type=jnp.float32)]
    reduce_sum x9 -> x0, other arithmetic: 15.6 us -> none  [the longest x1 7.07 us: per_device(): jnp.mean(widened * widened, axis=-1, keepdims=True) + 1e-05]
    all_to_all x1 -> x0, blocking collectives: 14.5 us -> none  [sent_to_all(): return lax.all_to_all(copies, axis, split_axis=0, concat_axis=0, tiled=True)]
    convert_element_type x4 -> x0, other arithmetic: 9 us -> none  [the longest x1 8.22 us: per_device(): normed = (widened * lax.rsqrt(jnp.mean(widened * widened, axis=-1, keepdi...]
    another operation x2 -> x0, other arithmetic: 5.66 us -> none
    cos x1 -> x0, other arithmetic: 4.3 us -> none  [rotate(): cosine = jnp.cos(angles)[:, None, :]]
  transfers between devices with their start and end apart: 1 -> 0, of which waited for: 1 -> 0; matrix products, arithmetic and copies ran while one was open for 0% -> 0% of each run, Pallas kernels for 0% -> 0%
where the time goes in v3:
time: 53.6 us; the launch traced here: 53.2 us
  Pallas kernels  49.4 us (92%)
  local copies, waits for them, and re-layouts  3.15 us (6%)
  between operations  0.64 us (1%)
    pallas_call x1, Pallas kernels, per_device(): pl.pallas_call(whole_kernel, out_shape=(jax.ShapeDtypeStruct((slots, WAYS...  49.4 us
    unnamed x2, local copies, waits for them, and re-layouts  3.15 us

profile of v3, /device:TPU:1, one launch (start us, length us, event | category | flops | bytes accessed | tf_op | source)
XLA Modules:
  0.0 53.2 jit_solution(15964063998214746886)
XLA Ops:
  0.6 49.4 %whole.1 = (f32[8,32]{1,0:T(8,128)}, f32[128,1024]{1,0:T(8,128)}) custom-call(s32[8]{0:T(128)} %starts_h.1, s32[8]{0:T(128)} %lengths_h.1, s32[256]{0:T(256)} %episode_h.1, s32[256]{0:T(256)} %class_h.1, s32[256]{0:T(256)} %flag_h.1, bf16[4096]{0:T(1024)(128)(2,1)} %gain_h.1, f32[2,64,128]{2,1,0:T(8,128)} %constant.4.clone.fine_h, ...), custom_call_target="tpu_custom_call" | custom-call | tf_op jit(solution)/shard_map/whole/pallas_call | solution.py:579
  50.1 1.3 %copy.17 = f32[8,32]{1,0:T(8,128)} copy(f32[8,32]{1,0:T(8,128)} %get-tuple-element.4) | data formatting | bytes 2048
  51.3 1.9 %copy.18 = f32[128,1024]{1,0:T(8,128)} copy(f32[128,1024]{1,0:T(8,128)} %get-tuple-element.5) | data formatting | bytes 1048576

commit v4 on v3

v4 whole, which is shorter than its diff:
```python
import functools
import math

import jax
import jax.numpy as jnp
import numpy as np
from jax import lax
from jax.experimental import pallas as pl
from jax.experimental.pallas import tpu as pltpu
from jax.sharding import PartitionSpec as P

HEAD_DIM = 128
WAYS = 32
ROPE_BASE = 500000.0
LONGEST = 640
STEPS = 8
AHEAD = 3
TILE = 128
ONES = 16
EARLY = 4
PIECES = 2
BLOCK = 512
SHORTEST = 128
FAR = -(2.0**100)
F32 = jnp.float32
BF16 = jnp.bfloat16


def rope_tables(rows, block):
    half = HEAD_DIM // 2
    frequency = ROPE_BASE ** (-(np.arange(half, dtype=np.float64) * 2.0 / HEAD_DIM))
    frequency = np.concatenate([frequency, frequency])[None, :]
    sign = np.where(np.arange(HEAD_DIM) < half, -1.0, 1.0)[None, :]
    fine = np.arange(block, dtype=np.float64)[:, None] * frequency
    coarse = np.arange(0, rows, block, dtype=np.float64)[:, None] * frequency
    fine_table = np.stack([np.cos(fine), np.sin(fine)])
    coarse_table = np.stack(
        [np.cos(coarse), np.sin(coarse), sign * np.cos(coarse), sign * np.sin(coarse)]
    )
    return fine_table.astype(np.float32), coarse_table.astype(np.float32)


def dot(a, b):
    return jnp.dot(a, b, preferred_element_type=F32)


def dot_nt(a, b):
    return lax.dot_general(a, b, (((1,), (1,)), ((), ())), preferred_element_type=F32)


def split(a):
    high = a.astype(BF16)
    return high, (a - high.astype(F32)).astype(BF16)


def fold(a):
    span = a.shape[1] // PIECES
    return jnp.concatenate([a[:, p * span : (p + 1) * span] for p in range(PIECES)], axis=0)


def unfold(a, before, after):
    axis = a.ndim - 2
    size = a.shape[axis] // PIECES
    pad = lambda n: [jnp.zeros(a.shape[:axis] + (n, a.shape[-1]), a.dtype)] if n else []
    pieces = [
        jnp.concatenate(
            pad(before)
            + [lax.slice_in_dim(a, p * size, (p + 1) * size, axis=axis)]
            + pad(after),
            axis=axis,
        )
        for p in range(PIECES)
    ]
    return jnp.concatenate(pieces, axis=axis + 1)


def whole_kernel(
    starts_h,
    lengths_h,
    episode_h,
    class_h,
    flag_h,
    gain_h,
    fine_h,
    coarse_h,
    x_h,
    wq_h,
    wk_h,
    wv_h,
    wo_h,
    log_ref,
    proto_ref,
    starts,
    lengths,
    episode_s,
    flag_s,
    episode_v,
    class_v,
    flag_v,
    gain,
    fine,
    coarse,
    x_v,
    w_v,
    wo_v,
    acc,
    squares,
    member,
    qt,
    ks,
    vt,
    ot,
    part,
    landed,
    everyone,
    late_part,
    late_landed,
    late_total,
    late_everyone,
    square_part,
    square_landed,
    final_part,
    final_landed,
    small_sem,
    x_sem,
    wq_sem,
    wk_sem,
    wv_sem,
    wo_sem,
    rs_send,
    rs_recv,
    ar_send,
    ar_recv,
    sq_send,
    sq_recv,
    ag_send,
    ag_recv,
    relay_send,
    relay_recv,
    fin_send,
    fin_recv,
):
    mp = lax.axis_size("mp")
    dp = lax.axis_size("dp")
    me = lax.axis_index("mp")
    mine = lax.axis_index("dp")
    rows, width = x_h.shape
    slots = starts.shape[0]
    heads = wq_h.shape[1] // HEAD_DIM
    depth = width // STEPS
    tiles = rows // TILE
    share = width // mp
    late = slots - EARLY
    late_rows = late
    cut = rows - late * SHORTEST
    late_from = EARLY * SHORTEST

    smalls = [
        pltpu.make_async_copy(source, target, small_sem.at[i])
        for i, (source, target) in enumerate(
            [
                (gain_h, gain),
                (starts_h, starts),
                (lengths_h, lengths),
                (fine_h, fine),
                (coarse_h, coarse),
                (episode_h, episode_s),
                (flag_h, flag_s),
                (episode_h, episode_v),
                (class_h, class_v),
                (flag_h, flag_v),
            ]
        )
    ]

    bounds = [(0, depth // 2), (depth // 2, depth // 2)]
    bounds += [(depth, depth)]
    bounds += [(c * depth, 2 * depth) for c in range(2, STEPS, 2)]

    def chunk_copies(c):
        at = pl.ds(*bounds[c])
        q, k = heads * HEAD_DIM, HEAD_DIM
        return [
            pltpu.make_async_copy(
                x_h.at[:, at], x_v.at[:, at], x_sem.at[c]
            ),
            pltpu.make_async_copy(wq_h.at[at, :], w_v.at[at, pl.ds(0, q)], wq_sem.at[c]),
            pltpu.make_async_copy(wk_h.at[at, :], w_v.at[at, pl.ds(q, k)], wk_sem.at[c]),
            pltpu.make_async_copy(wv_h.at[at, :], w_v.at[at, pl.ds(q + k, k)], wv_sem.at[c]),
        ]

    smalls[0].start()
    for copy in chunk_copies(0):
        copy.start()
    for copy in smalls[1:]:
        copy.start()
    for c in range(1, AHEAD):
        for copy in chunk_copies(c):
            copy.start()
    wo_copy = pltpu.make_async_copy(wo_h, wo_v, wo_sem.at[0])

    def lane_squares(x):
        wide = x.astype(F32)
        wide = wide * wide
        total = wide[:, 0:128]
        for i in range(1, x.shape[1] // 128):
            total += wide[:, i * 128 : (i + 1) * 128]
        return total

    def project_chunk(c):
        deep = pl.ds(*bounds[c])
        for first in range(0, rows, BLOCK):
            at = pl.ds(first, BLOCK)
            x = x_v[at, deep]
            value = dot(x * gain[deep].reshape(1, bounds[c][1]), w_v[deep, :])
            if c == 0:
                squares[at, :] = lane_squares(x)
                acc[at, :] = value
            else:
                squares[at, :] += lane_squares(x)
                acc[at, :] += value

    scale = math.log2(math.e) / math.sqrt(HEAD_DIM)

    def row_scale_of(at):
        return lax.rsqrt(jnp.sum(squares[at, :], axis=1, keepdims=True) * (1.0 / width) + 1e-05)

    def slot_bounds(shape, axis):
        index = lax.broadcasted_iota(jnp.int32, shape, axis)
        first = jnp.full(shape, rows, jnp.int32)
        last = jnp.zeros(shape, jnp.int32)
        for s in range(slots):
            first = jnp.where(index == s, starts[s], first)
            last = jnp.where(index == s, starts[s] + lengths[s], last)
        return first, last

    def prepare(i):
        first, last = slot_bounds((1, 128), 1)
        fine_cos, fine_sin = fine[0], fine[1]
        at = pl.ds(i * TILE, TILE)
        row_scale = row_scale_of(at)
        cosines, sines = [], []
        for b in range(i * TILE // 64, (i + 1) * TILE // 64):
            cos_a, sin_a = coarse[0, b : b + 1, :], coarse[1, b : b + 1, :]
            cos_s, sin_s = coarse[2, b : b + 1, :], coarse[3, b : b + 1, :]
            cosines.append(cos_a * fine_cos - sin_a * fine_sin)
            sines.append(sin_s * fine_cos + cos_s * fine_sin)
        cosine = jnp.concatenate(cosines, axis=0) * row_scale
        sine = jnp.concatenate(sines, axis=0) * row_scale
        for n in range(heads):
            v = acc[at, n * 128 : (n + 1) * 128]
            v = v * cosine + pltpu.roll(v, 64, 1) * sine
            qt[i % 3, 0:128, n * TILE : (n + 1) * TILE] = v.T.astype(BF16)
            qt[i % 3, 128 : 128 + ONES, n * TILE : (n + 1) * TILE] = member[:, at]
        v = acc[at, heads * 128 : (heads + 1) * 128] * scale
        v = v * cosine + pltpu.roll(v, 64, 1) * sine
        ks[at, 0:128] = v.astype(BF16)
        token = i * TILE + lax.broadcasted_iota(jnp.int32, (TILE, 128), 0)
        inside = (token >= first) & (token < last)
        ks[at, 128:256] = jnp.where(inside, 0.0, FAR).astype(BF16)
        v = acc[at, (heads + 1) * 128 : (heads + 2) * 128] * row_scale
        vt[0:128, at] = v.T.astype(BF16)
        vt[128 : 128 + ONES, at] = jnp.ones((ONES, TILE), BF16)

    def score(i):
        begin = max(0, i * TILE - LONGEST)
        return dot(ks[begin : (i + 1) * TILE, :], qt[i % 3])

    def mix(i, s):
        key = lax.broadcasted_iota(jnp.int32, (TILE, heads * TILE), 0)
        query = lax.broadcasted_iota(jnp.int32, (TILE, heads * TILE), 1) % TILE
        begin = max(0, i * TILE - LONGEST)
        before = i * TILE - begin
        own = jnp.where(key <= query, s[before:], FAR)
        peak = jnp.max(own, axis=0, keepdims=True)
        if before:
            peak = jnp.maximum(peak, jnp.max(s[:before], axis=0, keepdims=True))
        e = jnp.exp2(own - peak).astype(BF16)
        if before:
            e = jnp.concatenate([jnp.exp2(s[:before] - peak).astype(BF16), e], axis=0)
        o = dot(vt[:, begin : (i + 1) * TILE], e)
        o = (o[0:128] / o[128:129]).astype(BF16)
        for n in range(heads):
            ot[n * 128 : (n + 1) * 128, i * TILE : (i + 1) * TILE] = o[:, n * TILE : (n + 1) * TILE]

    def attend(first, last):
        prepare(first)
        ready = score(first)
        for i in range(first, last):
            now = ready
            if i + 1 < last:
                prepare(i + 1)
                ready = score(i + 1)
            mix(i, now)

    def head_part(span, pick, target):
        high, low = split(dot_nt(member[:, span], ot[:, span])[pick])
        stacked = jnp.concatenate([high, low], axis=0)
        for r in range(mp):
            both = dot(stacked, wo_v[:, r * share : (r + 1) * share])
            n = both.shape[0] // 2
            target[r] = fold(both[:n] + both[n:])

    def divided(value, first, size):
        row = lax.broadcasted_iota(jnp.int32, (value.shape[0], 1), 0)
        count = jnp.ones(row.shape, jnp.int32)
        for s in range(value.shape[0]):
            count = jnp.where(row == s, lengths[first + s % size], count)
        return value / count.astype(F32)

    order = sorted(range(1, mp), key=lambda d: -min(d, mp - d))

    def to_ranks(source, target, send, recv):
        return {
            d: pltpu.make_async_remote_copy(
                src_ref=source(d),
                dst_ref=target.at[d - 1],
                send_sem=send.at[d - 1],
                recv_sem=recv.at[d - 1],
                device_id={"mp": (me + d) % mp},
            )
            for d in order
        }

    side = int(math.isqrt(dp // 2))
    x, y, core = mine // (2 * side), (mine // 2) % side, mine % 2
    partner = mine + 1 - 2 * core

    def at_offset(dx, dy):
        return (((x + dx + side) % side) * side + (y + dy + side) % side) * 2 + core

    reach = lambda o: min(o[0], side - o[0]) + min(o[1], side - o[1])
    offsets = [(dx, dy) for dx in range(side) for dy in range(side) if dx or dy]
    offsets = sorted(offsets, key=lambda o: -reach(o))

    gathered = (everyone, late_everyone)

    def gather_copy(group, i):
        return pltpu.make_async_remote_copy(
            src_ref=gathered[group].at[mine],
            dst_ref=gathered[group].at[mine],
            send_sem=ag_send.at[group, i],
            recv_sem=ag_recv.at[group, i],
            device_id={"dp": at_offset(*offsets[i])},
        )

    def relay_copy(group, i):
        source = mine if i == len(offsets) else at_offset(-offsets[i][0], -offsets[i][1])
        return pltpu.make_async_remote_copy(
            src_ref=gathered[group].at[source],
            dst_ref=gathered[group].at[source],
            send_sem=relay_send.at[group, i],
            recv_sem=relay_recv.at[group, i],
            device_id={"dp": partner},
        )

    def gather(group):
        for i in range(len(offsets)):
            gather_copy(group, i).start()
        relay_copy(group, len(offsets)).start()

    def relay(group):
        for i in reversed(range(len(offsets))):
            gather_copy(group, i).wait_recv()
            relay_copy(group, i).start()

    barrier = pltpu.get_barrier_semaphore()
    for d in range(1, mp):
        pl.semaphore_signal(barrier, inc=1, device_id={"mp": (me + d) % mp})
    for offset in offsets:
        pl.semaphore_signal(barrier, inc=1, device_id={"dp": at_offset(*offset)})
    pl.semaphore_signal(barrier, inc=1, device_id={"dp": partner})
    smalls[0].wait()
    for c in range(len(bounds)):
        for copy in chunk_copies(c):
            copy.wait()
        if c + AHEAD < len(bounds):
            for copy in chunk_copies(c + AHEAD):
                copy.start()
        elif c + AHEAD == len(bounds):
            wo_copy.start()
        project_chunk(c)
    for copy in smalls[1:]:
        copy.wait()
    token = lax.broadcasted_iota(jnp.int32, (ONES, rows), 1)
    first, last = slot_bounds((ONES, rows), 0)
    member[...] = jnp.where((token >= first) & (token < last), 1.0, 0.0).astype(BF16)
    qt[:, 128 + ONES :, :] = jnp.zeros((3, 128 - ONES, heads * TILE), BF16)
    attend(0, cut // TILE)
    wo_copy.wait()
    head_part(slice(0, cut), slice(0, EARLY), part)
    pl.semaphore_wait(barrier, mp - 1 + len(offsets) + 1)
    reduce_early = to_ranks(lambda d: part.at[(me + d) % mp], landed, rs_send, rs_recv)
    for d in order:
        reduce_early[d].start()

    own_features = pl.ds(pl.multiple_of(me * share, share), share)
    pooled = fold(dot(member[:, :cut], x_v[:cut, own_features])[:EARLY])
    attend(cut // TILE, tiles)
    head_part(slice(late_from, rows), slice(EARLY, slots), late_part)
    reduce_late = to_ranks(lambda d: late_part, late_landed, ar_send, ar_recv)
    for d in order:
        reduce_late[d].start()

    pooled += part[me]
    for d in reversed(order):
        reduce_early[d].wait_recv()
        pooled += landed[d - 1]
    pooled = divided(pooled, 0, EARLY)
    everyone[mine] = pooled
    gather(0)
    late_tokens = dot(member[:, late_from:], x_v[late_from:, :])[EARLY:slots]
    for r in range(mp):
        late_total[r] = fold(late_tokens[:, r * share : (r + 1) * share]) + late_part[r]
    total = dp * slots
    classes = proto_ref.shape[0]
    named = episode_v[...] * WAYS + class_v[...]
    named = jnp.where(flag_v[...] == 0, named, -1).reshape(1, total)
    kind = lax.broadcasted_iota(jnp.int32, (classes, total), 0)
    select = jnp.where(kind == named, 1.0, 0.0).astype(BF16)
    relay(0)
    for i in range(len(offsets) + 1):
        relay_copy(0, i).wait_recv()
    early = unfold(everyone[...], 0, late_rows)
    square = jnp.sum(early * early, axis=2, keepdims=True)
    wide_lane = lax.broadcasted_iota(jnp.int32, (dp, slots, 128), 2)
    wide_slot = lax.broadcasted_iota(jnp.int32, (dp, slots, 128), 1)
    square = jnp.sum(jnp.where(wide_lane == wide_slot, square, 0.0), axis=1)
    square_part[...] = square
    copies_sq = to_ranks(lambda d: square_part, square_landed, sq_send, sq_recv)
    for d in order:
        copies_sq[d].start()
    for d in reversed(order):
        reduce_late[d].wait_recv()
    late_square = jnp.zeros((late_rows * PIECES, 1), F32)
    for r in range(mp):
        value = late_total[r]
        for d in order:
            value += late_landed[d - 1, r]
        value = divided(value, EARLY, late_rows)
        late_total[r] = value
        late_square += jnp.sum(value * value, axis=1, keepdims=True)
    lane = lax.broadcasted_iota(jnp.int32, (slots, 128), 1)
    slot = lax.broadcasted_iota(jnp.int32, (slots, 128), 0)
    late_square = jnp.sum(
        jnp.where(lane % late_rows == slot % late_rows, late_square, 0.0), axis=0, keepdims=True
    )
    late_mean = jnp.sum(
        jnp.where(lane == slot % late_rows, late_square, 0.0), axis=1, keepdims=True
    ) * (1.0 / width)
    late_own = late_total[me] * lax.rsqrt(late_mean + 1e-06)
    late_everyone[mine] = late_own
    gather(1)

    for d in reversed(order):
        copies_sq[d].wait_recv()
        square += square_landed[d - 1]
    square_part_total = square.reshape(dp, 1, 128)
    mean = jnp.sum(
        jnp.where(wide_lane == wide_slot, square_part_total, 0.0), axis=2, keepdims=True
    ) * (1.0 / width)
    high, low = split((early * lax.rsqrt(mean + 1e-06)).reshape(total, share))
    sums = dot(select, high) + dot(select, low)
    own_row = lax.broadcasted_iota(jnp.int32, (dp, 128), 0) == mine
    own_square = jnp.sum(jnp.where(own_row, square, 0.0), axis=0, keepdims=True)
    own_square = jnp.where(slot >= EARLY, late_square, own_square)
    own_mean = jnp.sum(jnp.where(lane == slot, own_square, 0.0), axis=1, keepdims=True) * (
        1.0 / width
    )
    own_weight = lax.rsqrt(own_mean + 1e-06)
    own = unfold(pooled, 0, late_rows) * own_weight + unfold(late_own, EARLY, 0)
    own_high, own_low = split(own)
    own = jnp.concatenate([own_high, own_low], axis=0)
    relay(1)
    for i in range(len(offsets) + 1):
        relay_copy(1, i).wait_recv()
    high, low = split(unfold(late_everyone[...], EARLY, 0).reshape(total, share))
    sums += dot(select, high) + dot(select, low)
    sums_high, sums_low = split(sums)
    diagonal = lax.broadcasted_iota(jnp.int32, (classes, classes), 0) == lax.broadcasted_iota(
        jnp.int32, (classes, classes), 1
    )
    norms = jnp.sum(sums * sums, axis=1, keepdims=True)
    norms = jnp.sum(jnp.where(diagonal, norms, 0.0), axis=0, keepdims=True)
    cross = dot_nt(own, sums_high)
    cross = cross[:slots] + cross[slots:] + dot_nt(own, sums_low)[:slots]
    mixed = jnp.concatenate([cross, jnp.broadcast_to(norms, (slots, classes))], axis=0)
    final_part[...] = mixed
    copies_fin = to_ranks(lambda d: final_part, final_landed, fin_send, fin_recv)
    for d in order:
        copies_fin[d].start()
    for d in reversed(order):
        copies_fin[d].wait_recv()
        mixed += final_landed[d - 1]
    class_mean = mixed[slots : slots + 1] * (1.0 / width)
    class_scale = lax.rsqrt(class_mean + 1e-06)
    column = jnp.sum(jnp.where(diagonal, class_scale, 0.0), axis=1, keepdims=True)
    proto_ref[...] = sums * column
    distance = (
        own_mean * own_weight * own_weight + class_mean * class_scale * class_scale
    ) * width - 2.0 * (mixed[:slots] * class_scale)
    row = lax.broadcasted_iota(jnp.int32, (slots, 1), 0)
    episode = jnp.zeros((slots, 1), jnp.int32)
    asked = jnp.zeros((slots, 1), jnp.int32)
    for s in range(slots):
        episode = jnp.where(row == s, episode_s[mine * slots + s], episode)
        asked = jnp.where(row == s, flag_s[mine * slots + s], asked)
    picked = jnp.zeros((slots, WAYS), F32)
    for e in range(classes // WAYS):
        picked = jnp.where(episode == e, distance[:, e * WAYS : (e + 1) * WAYS], picked)
    logits = picked * (-1.0 / math.sqrt(width))
    shifted = logits - jnp.max(logits, axis=1, keepdims=True)
    result = shifted - jnp.log(jnp.sum(jnp.exp(shifted), axis=1, keepdims=True))
    log_ref[...] = jnp.where(asked == 1, result, 0.0)

    for copies in (reduce_early, reduce_late, copies_sq, copies_fin):
        for d in order:
            copies[d].wait_send()
    for group in range(2):
        for i in range(len(offsets)):
            gather_copy(group, i).wait_send()
        for i in range(len(offsets) + 1):
            relay_copy(group, i).wait_send()


def per_device(
    tokens,
    norm_gain,
    w_query,
    w_key,
    w_value,
    w_out,
    seq_starts,
    seq_lengths,
    episode_ids,
    class_ids,
    query_flags,
):
    rows, width = tokens.shape
    slots = seq_starts.shape[0]
    inner = w_query.shape[1]
    heads = inner // HEAD_DIM
    columns = inner + w_key.shape[1] + w_value.shape[1]
    mp, dp = lax.axis_size("mp"), lax.axis_size("dp")
    share = width // mp
    tiles = rows // TILE
    total = episode_ids.shape[0]
    classes = max(1, total // (2 * WAYS)) * WAYS
    chips = dp // 2
    late = (slots - EARLY) * PIECES
    fine, coarse = rope_tables(rows, 64)
    hbm = pl.BlockSpec(memory_space=pltpu.HBM)
    vmem = pl.BlockSpec(memory_space=pltpu.VMEM)
    dma = lambda *n: pltpu.SemaphoreType.DMA(n)
    ints = lambda n: pltpu.SMEM((n,), jnp.int32)
    return pl.pallas_call(
        whole_kernel,
        out_shape=(
            jax.ShapeDtypeStruct((slots, WAYS), F32),
            jax.ShapeDtypeStruct((classes, share), F32),
        ),
        in_specs=[hbm] * 13,
        out_specs=(vmem, vmem),
        scratch_shapes=[
            ints(slots),
            ints(slots),
            ints(total),
            ints(total),
            pltpu.VMEM((total,), jnp.int32),
            pltpu.VMEM((total,), jnp.int32),
            pltpu.VMEM((total,), jnp.int32),
            pltpu.VMEM((width,), BF16),
            pltpu.VMEM(fine.shape, F32),
            pltpu.VMEM(coarse.shape, F32),
            pltpu.VMEM((rows, width), BF16),
            pltpu.VMEM((width, columns), BF16),
            pltpu.VMEM((inner, width), BF16),
            pltpu.VMEM((rows, columns), F32),
            pltpu.VMEM((rows, 128), F32),
            pltpu.VMEM((ONES, rows), BF16),
            pltpu.VMEM((3, 256, heads * TILE), BF16),
            pltpu.VMEM((rows, 256), BF16),
            pltpu.VMEM((128 + ONES, rows), BF16),
            pltpu.VMEM((inner, rows), BF16),
            pltpu.VMEM((mp, EARLY * PIECES, share // PIECES), F32),
            pltpu.VMEM((mp - 1, EARLY * PIECES, share // PIECES), F32),
            pltpu.VMEM((dp, EARLY * PIECES, share // PIECES), F32),
            pltpu.VMEM((mp, late, share // PIECES), F32),
            pltpu.VMEM((mp - 1, mp, late, share // PIECES), F32),
            pltpu.VMEM((mp, late, share // PIECES), F32),
            pltpu.VMEM((dp, late, share // PIECES), F32),
            pltpu.VMEM((dp, 128), F32),
            pltpu.VMEM((mp - 1, dp, 128), F32),
            pltpu.VMEM((2 * slots, 128), F32),
            pltpu.VMEM((mp - 1, 2 * slots, 128), F32),
            dma(10),
            dma(STEPS + 1),
            dma(STEPS + 1),
            dma(STEPS + 1),
            dma(STEPS + 1),
            dma(1),
            dma(mp - 1),
            dma(mp - 1),
            dma(mp - 1),
            dma(mp - 1),
            dma(mp - 1),
            dma(mp - 1),
            dma(2, chips - 1),
            dma(2, chips - 1),
            dma(2, chips),
            dma(2, chips),
            dma(mp - 1),
            dma(mp - 1),
        ],
        compiler_params=pltpu.CompilerParams(
            collective_id=0, has_side_effects=True, vmem_limit_bytes=50 * 2**20
        ),
        name="whole",
    )(
        *(
            pltpu.with_memory_space_constraint(array, pltpu.HBM)
            for array in (
                seq_starts,
                seq_lengths,
                episode_ids,
                class_ids,
                query_flags,
                norm_gain,
                jnp.asarray(fine),
                jnp.asarray(coarse),
                tokens,
                w_query,
                w_key,
                w_value,
                w_out,
            )
        )
    )


def solution(mesh):
    placed = (
        P("dp", None),
        P(),
        P(None, "mp"),
        P(None, "mp"),
        P(None, "mp"),
        P("mp", None),
        P("dp"),
        P("dp"),
        P(),
        P(),
        P(),
    )
    return jax.shard_map(
        per_device,
        mesh=mesh,
        in_specs=placed,
        out_specs=(P("dp", None), P(None, "mp")),
        check_vma=False,
    )
```

time: 53.6 us -> 48.8 us (0.910)
  Pallas kernels: 49.4 us -> 46.7 us
  local copies, waits for them, and re-layouts: 3.15 us -> 1.39 us
    pallas_call x1, Pallas kernels: 49.4 us -> 46.7 us  [per_device(): pl.pallas_call(whole_kernel, out_shape=(jax.ShapeDtypeStruct((slots, WAYS...]
    unnamed x2, local copies, waits for them, and re-layouts: 3.15 us -> 1.39 us
where the time goes in v4:
time: 48.8 us; the launch traced here: 48.7 us
  Pallas kernels  46.7 us (96%)
  local copies, waits for them, and re-layouts  1.39 us (3%)
  between operations  0.64 us (1%)
    pallas_call x1, Pallas kernels, per_device(): pl.pallas_call(whole_kernel, out_shape=(jax.ShapeDtypeStruct((slots, WAYS...  46.7 us
    unnamed x2, local copies, waits for them, and re-layouts  1.39 us

profile of v4, /device:TPU:1, one launch (start us, length us, event | category | flops | bytes accessed | tf_op | source)
XLA Modules:
  0.0 48.7 jit_solution(2052148578236488074)
XLA Ops:
  0.6 46.7 %whole.1 = (f32[8,32]{1,0:T(8,128)S(1)}, f32[128,1024]{1,0:T(8,128)S(1)}) custom-call(s32[8]{0:T(128)} %starts_h.1, s32[8]{0:T(128)} %lengths_h.1, s32[256]{0:T(256)} %episode_h.1, s32[256]{0:T(256)} %class_h.1, s32[256]{0:T(256)} %flag_h.1, bf16[4096]{0:T(1024)(128)(2,1)} %gain_h.1, f32[2,64,128]{2,1,0:T(8,128)} %constant.4.clone.fine_h, ...), custom_call_target="tpu_custom_call" | custom-call | tf_op jit(solution)/shard_map/whole/pallas_call | solution.py:556
  47.3 0.6 %copy.17 = f32[8,32]{1,0:T(8,128)} copy(f32[8,32]{1,0:T(8,128)S(1)} %get-tuple-element.4) | data formatting | bytes 2048
  47.9 0.8 %copy.18 = f32[128,1024]{1,0:T(8,128)} copy(f32[128,1024]{1,0:T(8,128)S(1)} %get-tuple-element.5) | data formatting | bytes 1048576

commit v5 on v4

--- a/solution.py
+++ b/solution.py
@@ -14,7 +14,8 @@
 ROPE_BASE = 500000.0
 LONGEST = 640
 STEPS = 8
-AHEAD = 3
+AHEAD = 2
+HELD = 6
 TILE = 128
 ONES = 16
 EARLY = 4
@@ -58,20 +59,17 @@
     return jnp.concatenate([a[:, p * span : (p + 1) * span] for p in range(PIECES)], axis=0)
 
 
-def unfold(a, before, after):
-    axis = a.ndim - 2
-    size = a.shape[axis] // PIECES
-    pad = lambda n: [jnp.zeros(a.shape[:axis] + (n, a.shape[-1]), a.dtype)] if n else []
-    pieces = [
-        jnp.concatenate(
-            pad(before)
-            + [lax.slice_in_dim(a, p * size, (p + 1) * size, axis=axis)]
-            + pad(after),
-            axis=axis,
-        )
-        for p in range(PIECES)
-    ]
-    return jnp.concatenate(pieces, axis=axis + 1)
+def unfold(first, second):
+    axis = first.ndim - 2
+    size = first.shape[axis] // PIECES
+    piece = lambda a, p: lax.slice_in_dim(a, p * size, (p + 1) * size, axis=axis)
+    return jnp.concatenate(
+        [
+            jnp.concatenate([piece(first, p), piece(second, p)], axis=axis)
+            for p in range(PIECES)
+        ],
+        axis=axis + 1,
+    )
 
 
 def whole_kernel(
@@ -113,10 +111,6 @@
     part,
     landed,
     everyone,
-    late_part,
-    late_landed,
-    late_total,
-    late_everyone,
     square_part,
     square_landed,
     final_part,
@@ -129,8 +123,6 @@
     wo_sem,
     rs_send,
     rs_recv,
-    ar_send,
-    ar_recv,
     sq_send,
     sq_recv,
     ag_send,
@@ -151,7 +143,6 @@
     tiles = rows // TILE
     share = width // mp
     late = slots - EARLY
-    late_rows = late
     cut = rows - late * SHORTEST
     late_from = EARLY * SHORTEST
 
@@ -250,8 +241,8 @@
         for n in range(heads):
             v = acc[at, n * 128 : (n + 1) * 128]
             v = v * cosine + pltpu.roll(v, 64, 1) * sine
-            qt[i % 3, 0:128, n * TILE : (n + 1) * TILE] = v.T.astype(BF16)
-            qt[i % 3, 128 : 128 + ONES, n * TILE : (n + 1) * TILE] = member[:, at]
+            qt[i % HELD, 0:128, n * TILE : (n + 1) * TILE] = v.T.astype(BF16)
+            qt[i % HELD, 128 : 128 + ONES, n * TILE : (n + 1) * TILE] = member[:, at]
         v = acc[at, heads * 128 : (heads + 1) * 128] * scale
         v = v * cosine + pltpu.roll(v, 64, 1) * sine
         ks[at, 0:128] = v.astype(BF16)
@@ -264,7 +255,7 @@
 
     def score(i):
         begin = max(0, i * TILE - LONGEST)
-        return dot(ks[begin : (i + 1) * TILE, :], qt[i % 3])
+        return dot(ks[begin : (i + 1) * TILE, :], qt[i % HELD])
 
     def mix(i, s):
         key = lax.broadcasted_iota(jnp.int32, (TILE, heads * TILE), 0)
@@ -293,13 +284,17 @@
                 ready = score(i + 1)
             mix(i, now)
 
-    def head_part(span, pick, target):
+    spans = (slice(0, cut), slice(late_from, rows))
+    picks = (slice(0, EARLY), slice(EARLY, slots))
+
+    def head_part(group):
+        span, pick = spans[group], picks[group]
         high, low = split(dot_nt(member[:, span], ot[:, span])[pick])
         stacked = jnp.concatenate([high, low], axis=0)
         for r in range(mp):
             both = dot(stacked, wo_v[:, r * share : (r + 1) * share])
             n = both.shape[0] // 2
-            target[r] = fold(both[:n] + both[n:])
+            part[group, r] = fold(both[:n] + both[n:])
 
     def divided(value, first, size):
         row = lax.broadcasted_iota(jnp.int32, (value.shape[0], 1), 0)
@@ -314,9 +309,9 @@
         return {
             d: pltpu.make_async_remote_copy(
                 src_ref=source(d),
-                dst_ref=target.at[d - 1],
-                send_sem=send.at[d - 1],
-                recv_sem=recv.at[d - 1],
+                dst_ref=target(d),
+                send_sem=send(d),
+                recv_sem=recv(d),
                 device_id={"mp": (me + d) % mp},
             )
             for d in order
@@ -333,12 +328,72 @@
     offsets = [(dx, dy) for dx in range(side) for dy in range(side) if dx or dy]
     offsets = sorted(offsets, key=lambda o: -reach(o))
 
-    gathered = (everyone, late_everyone)
+    def reduce_copies(group):
+        return to_ranks(
+            lambda d: part.at[group, (me + d) % mp],
+            lambda d: landed.at[group, d - 1],
+            lambda d: rs_send.at[group, d - 1],
+            lambda d: rs_recv.at[group, d - 1],
+        )
+
+    def square_copies(group):
+        return to_ranks(
+            lambda d: square_part.at[group],
+            lambda d: square_landed.at[group, d - 1],
+            lambda d: sq_send.at[group, d - 1],
+            lambda d: sq_recv.at[group, d - 1],
+        )
+
+    def token_part(group):
+        own_features = pl.ds(pl.multiple_of(me * share, share), share)
+        return fold(dot(member[:, spans[group]], x_v[spans[group], own_features])[picks[group]])
+
+    lane = lax.broadcasted_iota(jnp.int32, (slots, 128), 1)
+    slot = lax.broadcasted_iota(jnp.int32, (slots, 128), 0)
+
+    def reduced(group, value, copies):
+        value += part[group, me]
+        for d in reversed(order):
+            copies[d].wait_recv()
+            value += landed[group, d - 1]
+        value = divided(value, group * EARLY, EARLY)
+        square = jnp.sum(value * value, axis=1, keepdims=True)
+        square = jnp.sum(
+            jnp.where(lane % EARLY == slot % EARLY, square, 0.0), axis=0, keepdims=True
+        )
+        square_part[group] = square
+        sent = square_copies(group)
+        for d in order:
+            sent[d].start()
+        return value, square, sent
+
+    def embedded(group, value, square, sent):
+        for d in reversed(order):
+            sent[d].wait_recv()
+            square += square_landed[group, d - 1]
+        mean = jnp.sum(jnp.where(lane == slot % EARLY, square, 0.0), axis=1, keepdims=True)
+        mean = mean * (1.0 / width)
+        value = value * lax.rsqrt(mean + 1e-06)
+        everyone[group, mine] = value
+        gather(group)
+        return value, mean
+
+    def class_part(group):
+        a = everyone[group]
+        high = a.astype(BF16).astype(F32)
+        both = unfold(high, a - high).astype(BF16).reshape(total, share)
+        lanes = lax.broadcasted_iota(jnp.int32, (1, total), 1) % slots
+        if group == 0:
+            names = jnp.where(lanes < EARLY, named, pltpu.roll(named, EARLY, 1))
+        else:
+            names = jnp.where(lanes >= EARLY, named, pltpu.roll(named, total - EARLY, 1))
+        kind = lax.broadcasted_iota(jnp.int32, (classes, total), 0)
+        return dot(jnp.where(kind == names, 1.0, 0.0).astype(BF16), both)
 
     def gather_copy(group, i):
         return pltpu.make_async_remote_copy(
-            src_ref=gathered[group].at[mine],
-            dst_ref=gathered[group].at[mine],
+            src_ref=everyone.at[group, mine],
+            dst_ref=everyone.at[group, mine],
             send_sem=ag_send.at[group, i],
             recv_sem=ag_recv.at[group, i],
             device_id={"dp": at_offset(*offsets[i])},
@@ -347,8 +402,8 @@
     def relay_copy(group, i):
         source = mine if i == len(offsets) else at_offset(-offsets[i][0], -offsets[i][1])
         return pltpu.make_async_remote_copy(
-            src_ref=gathered[group].at[source],
-            dst_ref=gathered[group].at[source],
+            src_ref=everyone.at[group, source],
+            dst_ref=everyone.at[group, source],
             send_sem=relay_send.at[group, i],
             recv_sem=relay_recv.at[group, i],
             device_id={"dp": partner},
@@ -385,97 +440,42 @@
     token = lax.broadcasted_iota(jnp.int32, (ONES, rows), 1)
     first, last = slot_bounds((ONES, rows), 0)
     member[...] = jnp.where((token >= first) & (token < last), 1.0, 0.0).astype(BF16)
-    qt[:, 128 + ONES :, :] = jnp.zeros((3, 128 - ONES, heads * TILE), BF16)
+    qt[:, 128 + ONES :, :] = jnp.zeros((HELD, 128 - ONES, heads * TILE), BF16)
     attend(0, cut // TILE)
     wo_copy.wait()
-    head_part(slice(0, cut), slice(0, EARLY), part)
+    head_part(0)
     pl.semaphore_wait(barrier, mp - 1 + len(offsets) + 1)
-    reduce_early = to_ranks(lambda d: part.at[(me + d) % mp], landed, rs_send, rs_recv)
+    reduce_early = reduce_copies(0)
     for d in order:
         reduce_early[d].start()
-
-    own_features = pl.ds(pl.multiple_of(me * share, share), share)
-    pooled = fold(dot(member[:, :cut], x_v[:cut, own_features])[:EARLY])
+    tokens_early = token_part(0)
     attend(cut // TILE, tiles)
-    head_part(slice(late_from, rows), slice(EARLY, slots), late_part)
-    reduce_late = to_ranks(lambda d: late_part, late_landed, ar_send, ar_recv)
+    head_part(1)
+    reduce_late = reduce_copies(1)
     for d in order:
         reduce_late[d].start()
-
-    pooled += part[me]
-    for d in reversed(order):
-        reduce_early[d].wait_recv()
-        pooled += landed[d - 1]
-    pooled = divided(pooled, 0, EARLY)
-    everyone[mine] = pooled
-    gather(0)
-    late_tokens = dot(member[:, late_from:], x_v[late_from:, :])[EARLY:slots]
-    for r in range(mp):
-        late_total[r] = fold(late_tokens[:, r * share : (r + 1) * share]) + late_part[r]
+    pooled_early, square_early, sent_early = reduced(0, tokens_early, reduce_early)
+    tokens_late = token_part(1)
     total = dp * slots
     classes = proto_ref.shape[0]
-    named = episode_v[...] * WAYS + class_v[...]
-    named = jnp.where(flag_v[...] == 0, named, -1).reshape(1, total)
-    kind = lax.broadcasted_iota(jnp.int32, (classes, total), 0)
-    select = jnp.where(kind == named, 1.0, 0.0).astype(BF16)
+    named = (episode_v[...] * WAYS + class_v[...]).reshape(1, total)
+    named = jnp.where(flag_v[...].reshape(1, total) == 0, named, -1)
+    own_early, mean_early = embedded(0, pooled_early, square_early, sent_early)
+    pooled_late, square_late, sent_late = reduced(1, tokens_late, reduce_late)
+    own_late, mean_late = embedded(1, pooled_late, square_late, sent_late)
     relay(0)
+    own = unfold(own_early, own_late)
+    own_mean = jnp.concatenate([mean_early[:EARLY], mean_late[:EARLY]], axis=0)
+    own_weight = lax.rsqrt(own_mean + 1e-06)
+    own_high, own_low = split(own)
+    own = jnp.concatenate([own_high, own_low], axis=0)
     for i in range(len(offsets) + 1):
         relay_copy(0, i).wait_recv()
-    early = unfold(everyone[...], 0, late_rows)
-    square = jnp.sum(early * early, axis=2, keepdims=True)
-    wide_lane = lax.broadcasted_iota(jnp.int32, (dp, slots, 128), 2)
-    wide_slot = lax.broadcasted_iota(jnp.int32, (dp, slots, 128), 1)
-    square = jnp.sum(jnp.where(wide_lane == wide_slot, square, 0.0), axis=1)
-    square_part[...] = square
-    copies_sq = to_ranks(lambda d: square_part, square_landed, sq_send, sq_recv)
-    for d in order:
-        copies_sq[d].start()
-    for d in reversed(order):
-        reduce_late[d].wait_recv()
-    late_square = jnp.zeros((late_rows * PIECES, 1), F32)
-    for r in range(mp):
-        value = late_total[r]
-        for d in order:
-            value += late_landed[d - 1, r]
-        value = divided(value, EARLY, late_rows)
-        late_total[r] = value
-        late_square += jnp.sum(value * value, axis=1, keepdims=True)
-    lane = lax.broadcasted_iota(jnp.int32, (slots, 128), 1)
-    slot = lax.broadcasted_iota(jnp.int32, (slots, 128), 0)
-    late_square = jnp.sum(
-        jnp.where(lane % late_rows == slot % late_rows, late_square, 0.0), axis=0, keepdims=True
-    )
-    late_mean = jnp.sum(
-        jnp.where(lane == slot % late_rows, late_square, 0.0), axis=1, keepdims=True
-    ) * (1.0 / width)
-    late_own = late_total[me] * lax.rsqrt(late_mean + 1e-06)
-    late_everyone[mine] = late_own
-    gather(1)
-
-    for d in reversed(order):
-        copies_sq[d].wait_recv()
-        square += square_landed[d - 1]
-    square_part_total = square.reshape(dp, 1, 128)
-    mean = jnp.sum(
-        jnp.where(wide_lane == wide_slot, square_part_total, 0.0), axis=2, keepdims=True
-    ) * (1.0 / width)
-    high, low = split((early * lax.rsqrt(mean + 1e-06)).reshape(total, share))
-    sums = dot(select, high) + dot(select, low)
-    own_row = lax.broadcasted_iota(jnp.int32, (dp, 128), 0) == mine
-    own_square = jnp.sum(jnp.where(own_row, square, 0.0), axis=0, keepdims=True)
-    own_square = jnp.where(slot >= EARLY, late_square, own_square)
-    own_mean = jnp.sum(jnp.where(lane == slot, own_square, 0.0), axis=1, keepdims=True) * (
-        1.0 / width
-    )
-    own_weight = lax.rsqrt(own_mean + 1e-06)
-    own = unfold(pooled, 0, late_rows) * own_weight + unfold(late_own, EARLY, 0)
-    own_high, own_low = split(own)
-    own = jnp.concatenate([own_high, own_low], axis=0)
+    sums = class_part(0)
     relay(1)
     for i in range(len(offsets) + 1):
         relay_copy(1, i).wait_recv()
-    high, low = split(unfold(late_everyone[...], EARLY, 0).reshape(total, share))
-    sums += dot(select, high) + dot(select, low)
+    sums += class_part(1)
     sums_high, sums_low = split(sums)
     diagonal = lax.broadcasted_iota(jnp.int32, (classes, classes), 0) == lax.broadcasted_iota(
         jnp.int32, (classes, classes), 1
@@ -486,7 +486,12 @@
     cross = cross[:slots] + cross[slots:] + dot_nt(own, sums_low)[:slots]
     mixed = jnp.concatenate([cross, jnp.broadcast_to(norms, (slots, classes))], axis=0)
     final_part[...] = mixed
-    copies_fin = to_ranks(lambda d: final_part, final_landed, fin_send, fin_recv)
+    copies_fin = to_ranks(
+        lambda d: final_part,
+        lambda d: final_landed.at[d - 1],
+        lambda d: fin_send.at[d - 1],
+        lambda d: fin_recv.at[d - 1],
+    )
     for d in order:
         copies_fin[d].start()
     for d in reversed(order):
@@ -513,7 +518,7 @@
     result = shifted - jnp.log(jnp.sum(jnp.exp(shifted), axis=1, keepdims=True))
     log_ref[...] = jnp.where(asked == 1, result, 0.0)
 
-    for copies in (reduce_early, reduce_late, copies_sq, copies_fin):
+    for copies in (reduce_early, reduce_late, sent_early, sent_late, copies_fin):
         for d in order:
             copies[d].wait_send()
     for group in range(2):
@@ -547,7 +552,6 @@
     total = episode_ids.shape[0]
     classes = max(1, total // (2 * WAYS)) * WAYS
     chips = dp // 2
-    late = (slots - EARLY) * PIECES
     fine, coarse = rope_tables(rows, 64)
     hbm = pl.BlockSpec(memory_space=pltpu.HBM)
     vmem = pl.BlockSpec(memory_space=pltpu.VMEM)
@@ -578,19 +582,15 @@
             pltpu.VMEM((rows, columns), F32),
             pltpu.VMEM((rows, 128), F32),
             pltpu.VMEM((ONES, rows), BF16),
-            pltpu.VMEM((3, 256, heads * TILE), BF16),
+            pltpu.VMEM((HELD, 256, heads * TILE), BF16),
             pltpu.VMEM((rows, 256), BF16),
             pltpu.VMEM((128 + ONES, rows), BF16),
             pltpu.VMEM((inner, rows), BF16),
-            pltpu.VMEM((mp, EARLY * PIECES, share // PIECES), F32),
-            pltpu.VMEM((mp - 1, EARLY * PIECES, share // PIECES), F32),
-            pltpu.VMEM((dp, EARLY * PIECES, share // PIECES), F32),
-            pltpu.VMEM((mp, late, share // PIECES), F32),
-            pltpu.VMEM((mp - 1, mp, late, share // PIECES), F32),
-            pltpu.VMEM((mp, late, share // PIECES), F32),
-            pltpu.VMEM((dp, late, share // PIECES), F32),
-            pltpu.VMEM((dp, 128), F32),
-            pltpu.VMEM((mp - 1, dp, 128), F32),
+            pltpu.VMEM((2, mp, slots, share // PIECES), F32),
+            pltpu.VMEM((2, mp - 1, slots, share // PIECES), F32),
+            pltpu.VMEM((2, dp, slots, share // PIECES), F32),
+            pltpu.VMEM((2, 1, 128), F32),
+            pltpu.VMEM((2, mp - 1, 1, 128), F32),
             pltpu.VMEM((2 * slots, 128), F32),
             pltpu.VMEM((mp - 1, 2 * slots, 128), F32),
             dma(10),
@@ -599,12 +599,10 @@
             dma(STEPS + 1),
             dma(STEPS + 1),
             dma(1),
-            dma(mp - 1),
-            dma(mp - 1),
-            dma(mp - 1),
-            dma(mp - 1),
-            dma(mp - 1),
-            dma(mp - 1),
+            dma(2, mp - 1),
+            dma(2, mp - 1),
+            dma(2, mp - 1),
+            dma(2, mp - 1),
             dma(2, chips - 1),
             dma(2, chips - 1),
             dma(2, chips),

time: 48.8 us -> 49.8 us (1.020)
  Pallas kernels: 46.7 us -> 47.6 us
    pallas_call x1, Pallas kernels: 46.7 us -> 47.6 us  [per_device(): pl.pallas_call(whole_kernel, out_shape=(jax.ShapeDtypeStruct((slots, WAYS...]
where the time goes in v5:
time: 49.8 us; the launch traced here: 49.7 us
  Pallas kernels  47.6 us (96%)
  local copies, waits for them, and re-layouts  1.39 us (3%)
  between operations  0.64 us (1%)
    pallas_call x1, Pallas kernels, per_device(): pl.pallas_call(whole_kernel, out_shape=(jax.ShapeDtypeStruct((slots, WAYS...  47.6 us
    unnamed x2, local copies, waits for them, and re-layouts  1.39 us

profile of v5, /device:TPU:1, one launch (start us, length us, event | category | flops | bytes accessed | tf_op | source)
XLA Modules:
  0.0 49.7 jit_solution(9533951860385823964)
XLA Ops:
  0.6 47.6 %whole.1 = (f32[8,32]{1,0:T(8,128)S(1)}, f32[128,1024]{1,0:T(8,128)S(1)}) custom-call(s32[8]{0:T(128)} %starts_h.1, s32[8]{0:T(128)} %lengths_h.1, s32[256]{0:T(256)} %episode_h.1, s32[256]{0:T(256)} %class_h.1, s32[256]{0:T(256)} %flag_h.1, bf16[4096]{0:T(1024)(128)(2,1)} %gain_h.1, f32[2,64,128]{2,1,0:T(8,128)} %constant.4.clone.fine_h, ...), custom_call_target="tpu_custom_call" | custom-call | tf_op jit(solution)/shard_map/whole/pallas_call | solution.py:560
  48.3 0.6 %copy.17 = f32[8,32]{1,0:T(8,128)} copy(f32[8,32]{1,0:T(8,128)S(1)} %get-tuple-element.4) | data formatting | bytes 2048
  48.9 0.8 %copy.18 = f32[128,1024]{1,0:T(8,128)} copy(f32[128,1024]{1,0:T(8,128)S(1)} %get-tuple-element.5) | data formatting | bytes 1048576

commit v6 on v4

--- a/solution.py
+++ b/solution.py
@@ -15,6 +15,7 @@
 LONGEST = 640
 STEPS = 8
 AHEAD = 3
+HELD = 12
 TILE = 128
 ONES = 16
 EARLY = 4
@@ -89,7 +90,8 @@
     wv_h,
     wo_h,
     log_ref,
-    proto_ref,
+    sums_ref,
+    column_ref,
     starts,
     lengths,
     episode_s,
@@ -250,8 +252,8 @@
         for n in range(heads):
             v = acc[at, n * 128 : (n + 1) * 128]
             v = v * cosine + pltpu.roll(v, 64, 1) * sine
-            qt[i % 3, 0:128, n * TILE : (n + 1) * TILE] = v.T.astype(BF16)
-            qt[i % 3, 128 : 128 + ONES, n * TILE : (n + 1) * TILE] = member[:, at]
+            qt[i % HELD, 0:128, n * TILE : (n + 1) * TILE] = v.T.astype(BF16)
+            qt[i % HELD, 128 : 128 + ONES, n * TILE : (n + 1) * TILE] = member[:, at]
         v = acc[at, heads * 128 : (heads + 1) * 128] * scale
         v = v * cosine + pltpu.roll(v, 64, 1) * sine
         ks[at, 0:128] = v.astype(BF16)
@@ -264,7 +266,7 @@
 
     def score(i):
         begin = max(0, i * TILE - LONGEST)
-        return dot(ks[begin : (i + 1) * TILE, :], qt[i % 3])
+        return dot(ks[begin : (i + 1) * TILE, :], qt[i % HELD])
 
     def mix(i, s):
         key = lax.broadcasted_iota(jnp.int32, (TILE, heads * TILE), 0)
@@ -385,7 +387,7 @@
     token = lax.broadcasted_iota(jnp.int32, (ONES, rows), 1)
     first, last = slot_bounds((ONES, rows), 0)
     member[...] = jnp.where((token >= first) & (token < last), 1.0, 0.0).astype(BF16)
-    qt[:, 128 + ONES :, :] = jnp.zeros((3, 128 - ONES, heads * TILE), BF16)
+    qt[:, 128 + ONES :, :] = jnp.zeros((HELD, 128 - ONES, heads * TILE), BF16)
     attend(0, cut // TILE)
     wo_copy.wait()
     head_part(slice(0, cut), slice(0, EARLY), part)
@@ -413,23 +415,11 @@
     for r in range(mp):
         late_total[r] = fold(late_tokens[:, r * share : (r + 1) * share]) + late_part[r]
     total = dp * slots
-    classes = proto_ref.shape[0]
+    classes = sums_ref.shape[0]
     named = episode_v[...] * WAYS + class_v[...]
     named = jnp.where(flag_v[...] == 0, named, -1).reshape(1, total)
     kind = lax.broadcasted_iota(jnp.int32, (classes, total), 0)
     select = jnp.where(kind == named, 1.0, 0.0).astype(BF16)
-    relay(0)
-    for i in range(len(offsets) + 1):
-        relay_copy(0, i).wait_recv()
-    early = unfold(everyone[...], 0, late_rows)
-    square = jnp.sum(early * early, axis=2, keepdims=True)
-    wide_lane = lax.broadcasted_iota(jnp.int32, (dp, slots, 128), 2)
-    wide_slot = lax.broadcasted_iota(jnp.int32, (dp, slots, 128), 1)
-    square = jnp.sum(jnp.where(wide_lane == wide_slot, square, 0.0), axis=1)
-    square_part[...] = square
-    copies_sq = to_ranks(lambda d: square_part, square_landed, sq_send, sq_recv)
-    for d in order:
-        copies_sq[d].start()
     for d in reversed(order):
         reduce_late[d].wait_recv()
     late_square = jnp.zeros((late_rows * PIECES, 1), F32)
@@ -452,6 +442,19 @@
     late_everyone[mine] = late_own
     gather(1)
 
+    relay(0)
+    for i in range(len(offsets) + 1):
+        relay_copy(0, i).wait_recv()
+    early = unfold(everyone[...], 0, late_rows)
+    square = jnp.sum(early * early, axis=2, keepdims=True)
+    wide_lane = lax.broadcasted_iota(jnp.int32, (dp, slots, 128), 2)
+    wide_slot = lax.broadcasted_iota(jnp.int32, (dp, slots, 128), 1)
+    square = jnp.sum(jnp.where(wide_lane == wide_slot, square, 0.0), axis=1)
+    square_part[...] = square
+    copies_sq = to_ranks(lambda d: square_part, square_landed, sq_send, sq_recv)
+    for d in order:
+        copies_sq[d].start()
+    relay(1)
     for d in reversed(order):
         copies_sq[d].wait_recv()
         square += square_landed[d - 1]
@@ -471,7 +474,6 @@
     own = unfold(pooled, 0, late_rows) * own_weight + unfold(late_own, EARLY, 0)
     own_high, own_low = split(own)
     own = jnp.concatenate([own_high, own_low], axis=0)
-    relay(1)
     for i in range(len(offsets) + 1):
         relay_copy(1, i).wait_recv()
     high, low = split(unfold(late_everyone[...], EARLY, 0).reshape(total, share))
@@ -489,13 +491,14 @@
     copies_fin = to_ranks(lambda d: final_part, final_landed, fin_send, fin_recv)
     for d in order:
         copies_fin[d].start()
+    sums_ref[...] = sums
     for d in reversed(order):
         copies_fin[d].wait_recv()
         mixed += final_landed[d - 1]
     class_mean = mixed[slots : slots + 1] * (1.0 / width)
     class_scale = lax.rsqrt(class_mean + 1e-06)
     column = jnp.sum(jnp.where(diagonal, class_scale, 0.0), axis=1, keepdims=True)
-    proto_ref[...] = sums * column
+    column_ref[...] = jnp.broadcast_to(column, column_ref.shape)
     distance = (
         own_mean * own_weight * own_weight + class_mean * class_scale * class_scale
     ) * width - 2.0 * (mixed[:slots] * class_scale)
@@ -521,6 +524,14 @@
             gather_copy(group, i).wait_send()
         for i in range(len(offsets) + 1):
             relay_copy(group, i).wait_send()
+
+
+def deliver_kernel(log_in, sums, column, log_ref, proto_ref):
+    log_ref[...] = log_in[...]
+    scale = column[...]
+    for c in range(0, sums.shape[1], scale.shape[1]):
+        at = pl.ds(c, scale.shape[1])
+        proto_ref[:, at] = sums[:, at] * scale
 
 
 def per_device(
@@ -553,14 +564,15 @@
     vmem = pl.BlockSpec(memory_space=pltpu.VMEM)
     dma = lambda *n: pltpu.SemaphoreType.DMA(n)
     ints = lambda n: pltpu.SMEM((n,), jnp.int32)
-    return pl.pallas_call(
+    log_probs, sums, column = pl.pallas_call(
         whole_kernel,
         out_shape=(
             jax.ShapeDtypeStruct((slots, WAYS), F32),
             jax.ShapeDtypeStruct((classes, share), F32),
+            jax.ShapeDtypeStruct((classes, 128), F32),
         ),
         in_specs=[hbm] * 13,
-        out_specs=(vmem, vmem),
+        out_specs=(vmem, vmem, vmem),
         scratch_shapes=[
             ints(slots),
             ints(slots),
@@ -578,7 +590,7 @@
             pltpu.VMEM((rows, columns), F32),
             pltpu.VMEM((rows, 128), F32),
             pltpu.VMEM((ONES, rows), BF16),
-            pltpu.VMEM((3, 256, heads * TILE), BF16),
+            pltpu.VMEM((HELD, 256, heads * TILE), BF16),
             pltpu.VMEM((rows, 256), BF16),
             pltpu.VMEM((128 + ONES, rows), BF16),
             pltpu.VMEM((inner, rows), BF16),
@@ -636,6 +648,17 @@
             )
         )
     )
+    return pl.pallas_call(
+        deliver_kernel,
+        out_shape=(
+            jax.ShapeDtypeStruct((slots, WAYS), F32),
+            jax.ShapeDtypeStruct((classes, share), F32),
+        ),
+        in_specs=[vmem] * 3,
+        out_specs=(vmem, vmem),
+        compiler_params=pltpu.CompilerParams(vmem_limit_bytes=8 * 2**20),
+        name="deliver",
+    )(log_probs, sums, column)
 
 
 def solution(mesh):

time: 48.8 us -> 47 us (0.963)
  local copies, waits for them, and re-layouts: 1.39 us -> 0 us
    unnamed x2 -> x0, local copies, waits for them, and re-layouts: 1.39 us -> none
    pallas_call x1, Pallas kernels: 46.7 us -> 45.4 us  [per_device(): pl.pallas_call(whole_kernel, out_shape=(jax.ShapeDtypeStruct((slots, WAYS...]
    pallas_call x0 -> x1, Pallas kernels: none -> 0.85 us  [per_device(): pl.pallas_call(deliver_kernel, out_shape=(jax.ShapeDtypeStruct((slots, WA...]
where the time goes in v6:
time: 47 us; the launch traced here: 46.9 us
  Pallas kernels  46.3 us (99%)
  between operations  0.64 us (1%)
    pallas_call x1, Pallas kernels, per_device(): pl.pallas_call(whole_kernel, out_shape=(jax.ShapeDtypeStruct((slots, WAYS...  45.4 us

profile of v6, /device:TPU:1, one launch (start us, length us, event | category | flops | bytes accessed | tf_op | source)
XLA Modules:
  0.0 46.9 jit_solution(4250481973824907449)
XLA Ops:
  0.6 45.4 %whole.1 = (f32[8,32]{1,0:T(8,128)S(1)}, f32[128,1024]{1,0:T(8,128)S(1)}, f32[128,128]{1,0:T(8,128)S(1)}) custom-call(s32[8]{0:T(128)} %starts_h.1, s32[8]{0:T(128)} %lengths_h.1, s32[256]{0:T(256)} %episode_h.1, s32[256]{0:T(256)} %class_h.1, s32[256]{0:T(256)} %flag_h.1, bf16[4096]{0:T(1024)(128)(2,1)} %gain_h.1, f32[2,64,128]{2,1,0:T(8,128)} %constant.4.clone.fine_h, ...), custom_call_target="tpu_custom_call" | custom-call | tf_op jit(solution)/shard_map/whole/pallas_call | solution.py:567
  46.1 0.8 %deliver.1 = (f32[8,32]{1,0:T(8,128)}, f32[128,1024]{1,0:T(8,128)}) custom-call(f32[8,32]{1,0:T(8,128)S(1)} %get-tuple-element.5.log_in, f32[128,1024]{1,0:T(8,128)S(1)} %get-tuple-element.6.sums, f32[128,128]{1,0:T(8,128)S(1)} %get-tuple-element.7.column), custom_call_target="tpu_custom_call" | custom-call | tf_op jit(solution)/shard_map/deliver/pallas_call | solution.py:651

commit v7 on v6

--- a/solution.py
+++ b/solution.py
@@ -492,6 +492,20 @@
     for d in order:
         copies_fin[d].start()
     sums_ref[...] = sums
+    row = lax.broadcasted_iota(jnp.int32, (slots, 1), 0)
+    episode = jnp.zeros((slots, 1), jnp.int32)
+    asked = jnp.zeros((slots, 1), jnp.int32)
+    for s in range(slots):
+        episode = jnp.where(row == s, episode_s[mine * slots + s], episode)
+        asked = jnp.where(row == s, flag_s[mine * slots + s], asked)
+    for copies in (reduce_early, reduce_late, copies_sq):
+        for d in order:
+            copies[d].wait_send()
+    for group in range(2):
+        for i in range(len(offsets)):
+            gather_copy(group, i).wait_send()
+        for i in range(len(offsets) + 1):
+            relay_copy(group, i).wait_send()
     for d in reversed(order):
         copies_fin[d].wait_recv()
         mixed += final_landed[d - 1]
@@ -502,12 +516,6 @@
     distance = (
         own_mean * own_weight * own_weight + class_mean * class_scale * class_scale
     ) * width - 2.0 * (mixed[:slots] * class_scale)
-    row = lax.broadcasted_iota(jnp.int32, (slots, 1), 0)
-    episode = jnp.zeros((slots, 1), jnp.int32)
-    asked = jnp.zeros((slots, 1), jnp.int32)
-    for s in range(slots):
-        episode = jnp.where(row == s, episode_s[mine * slots + s], episode)
-        asked = jnp.where(row == s, flag_s[mine * slots + s], asked)
     picked = jnp.zeros((slots, WAYS), F32)
     for e in range(classes // WAYS):
         picked = jnp.where(episode == e, distance[:, e * WAYS : (e + 1) * WAYS], picked)
@@ -516,14 +524,8 @@
     result = shifted - jnp.log(jnp.sum(jnp.exp(shifted), axis=1, keepdims=True))
     log_ref[...] = jnp.where(asked == 1, result, 0.0)
 
-    for copies in (reduce_early, reduce_late, copies_sq, copies_fin):
-        for d in order:
-            copies[d].wait_send()
-    for group in range(2):
-        for i in range(len(offsets)):
-            gather_copy(group, i).wait_send()
-        for i in range(len(offsets) + 1):
-            relay_copy(group, i).wait_send()
+    for d in order:
+        copies_fin[d].wait_send()
 
 
 def deliver_kernel(log_in, sums, column, log_ref, proto_ref):

time: 47 us -> 46.9 us (level)
  no operation moved by 1% of the time
where the time goes in v7:
time: 46.9 us; the launch traced here: 46.8 us
  Pallas kernels  46.2 us (99%)
  between operations  0.64 us (1%)
    pallas_call x1, Pallas kernels, per_device(): pl.pallas_call(whole_kernel, out_shape=(jax.ShapeDtypeStruct((slots, WAYS...  45.3 us

profile of v7, /device:TPU:1, one launch (start us, length us, event | category | flops | bytes accessed | tf_op | source)
XLA Modules:
  0.0 46.8 jit_solution(10163812803698469237)
XLA Ops:
  0.6 45.3 %whole.1 = (f32[8,32]{1,0:T(8,128)S(1)}, f32[128,1024]{1,0:T(8,128)S(1)}, f32[128,128]{1,0:T(8,128)S(1)}) custom-call(s32[8]{0:T(128)} %starts_h.1, s32[8]{0:T(128)} %lengths_h.1, s32[256]{0:T(256)} %episode_h.1, s32[256]{0:T(256)} %class_h.1, s32[256]{0:T(256)} %flag_h.1, bf16[4096]{0:T(1024)(128)(2,1)} %gain_h.1, f32[2,64,128]{2,1,0:T(8,128)} %constant.4.clone.fine_h, ...), custom_call_target="tpu_custom_call" | custom-call | tf_op jit(solution)/shard_map/whole/pallas_call | solution.py:569
  45.9 0.8 %deliver.1 = (f32[8,32]{1,0:T(8,128)}, f32[128,1024]{1,0:T(8,128)}) custom-call(f32[8,32]{1,0:T(8,128)S(1)} %get-tuple-element.5.log_in, f32[128,1024]{1,0:T(8,128)S(1)} %get-tuple-element.6.sums, f32[128,128]{1,0:T(8,128)S(1)} %get-tuple-element.7.column), custom_call_target="tpu_custom_call" | custom-call | tf_op jit(solution)/shard_map/deliver/pallas_call | solution.py:653

commit v8 on v7

--- a/solution.py
+++ b/solution.py
@@ -396,14 +396,14 @@
     for d in order:
         reduce_early[d].start()
 
-    own_features = pl.ds(pl.multiple_of(me * share, share), share)
-    pooled = fold(dot(member[:, :cut], x_v[:cut, own_features])[:EARLY])
     attend(cut // TILE, tiles)
     head_part(slice(late_from, rows), slice(EARLY, slots), late_part)
     reduce_late = to_ranks(lambda d: late_part, late_landed, ar_send, ar_recv)
     for d in order:
         reduce_late[d].start()
 
+    own_features = pl.ds(pl.multiple_of(me * share, share), share)
+    pooled = fold(dot(member[:, :cut], x_v[:cut, own_features])[:EARLY])
     pooled += part[me]
     for d in reversed(order):
         reduce_early[d].wait_recv()

time: 46.9 us -> 46.8 us (level)
  no operation moved by 1% of the time
where the time goes in v8:
time: 46.8 us; the launch traced here: 46.7 us
  Pallas kernels  46.1 us (99%)
  between operations  0.64 us (1%)
    pallas_call x1, Pallas kernels, per_device(): pl.pallas_call(whole_kernel, out_shape=(jax.ShapeDtypeStruct((slots, WAYS...  45.2 us

profile of v8, /device:TPU:1, one launch (start us, length us, event | category | flops | bytes accessed | tf_op | source)
XLA Modules:
  0.0 46.7 jit_solution(6933045715508060428)
XLA Ops:
  0.6 45.2 %whole.1 = (f32[8,32]{1,0:T(8,128)S(1)}, f32[128,1024]{1,0:T(8,128)S(1)}, f32[128,128]{1,0:T(8,128)S(1)}) custom-call(s32[8]{0:T(128)} %starts_h.1, s32[8]{0:T(128)} %lengths_h.1, s32[256]{0:T(256)} %episode_h.1, s32[256]{0:T(256)} %class_h.1, s32[256]{0:T(256)} %flag_h.1, bf16[4096]{0:T(1024)(128)(2,1)} %gain_h.1, f32[2,64,128]{2,1,0:T(8,128)} %constant.4.clone.fine_h, ...), custom_call_target="tpu_custom_call" | custom-call | tf_op jit(solution)/shard_map/whole/pallas_call | solution.py:569
  45.9 0.8 %deliver.1 = (f32[8,32]{1,0:T(8,128)}, f32[128,1024]{1,0:T(8,128)}) custom-call(f32[8,32]{1,0:T(8,128)S(1)} %get-tuple-element.5.log_in, f32[128,1024]{1,0:T(8,128)S(1)} %get-tuple-element.6.sums, f32[128,128]{1,0:T(8,128)S(1)} %get-tuple-element.7.column), custom_call_target="tpu_custom_call" | custom-call | tf_op jit(solution)/shard_map/deliver/pallas_call | solution.py:653
